TPU v7x, 16 devices: a whole 2x2x2 slice. The times are simulated.
16 devices in a mesh: my: 2 (over z), mx: 8 (over y, x, core).
Axes of the slice: x: 2, y: 2, z: 2, core: 2. Of those that a mesh axis runs over, the one named last changes fastest.
Arguments:
- x_in: bfloat16 [64, 5120], P(None, 'mx')
- seq_lens: int32 [64], P('mx')
- gain_attn: bfloat16 [5120], P('mx')
- gain_mlp: bfloat16 [5120], P('mx')
- w_q: bfloat16 [5120, 5120], P('mx', 'my')
- b_q: bfloat16 [5120], P('my')
- w_k: bfloat16 [5120, 1024], P('mx', 'my')
- b_k: bfloat16 [1024], P('my')
- w_v: bfloat16 [5120, 1024], P('mx', 'my')
- b_v: bfloat16 [1024], P('my')
- w_o: bfloat16 [5120, 5120], P('my', 'mx')
- w_gate: bfloat16 [5120, 27648], P('mx', 'my')
- w_up: bfloat16 [5120, 27648], P('mx', 'my')
- w_down: bfloat16 [27648, 5120], P('my', 'mx')
- k_cache: bfloat16 [64, 1024, 8, 128], P('mx', None, 'my')
- v_cache: bfloat16 [64, 1024, 8, 128], P('mx', None, 'my')
Outputs:
- output 1: bfloat16 [64, 5120], P(None, 'mx')
- output 2: bfloat16 [64, 1024, 8, 128], P('mx', None, 'my')
- output 3: bfloat16 [64, 1024, 8, 128], P('mx', None, 'my')
All inputs are finite; a program needn't handle non-finite values.
Results may differ from a plain program's by a relative error of at most 0.016982.
Values are sent between devices in bfloat16 or wider.
A program may use at most 1 GiB of HBM per device.

v0:
```python
import jax
import jax.numpy as jnp
from jax import lax
from jax.sharding import PartitionSpec as P

HEAD = 128
NORM_EPS = 1e-6
ROPE_THETA = 1000000.0


def apply_rotary(vectors, positions):
    half_dim = HEAD // 2
    inv_freq = ROPE_THETA ** (-2.0 * jnp.arange(half_dim, dtype=jnp.float32) / HEAD)
    angles = positions.astype(jnp.float32)[:, None, None] * inv_freq
    cos_tab = jnp.cos(angles)
    sin_tab = jnp.sin(angles)
    lower_half = vectors[..., :half_dim]
    upper_half = vectors[..., half_dim:]
    return jnp.concatenate([lower_half * cos_tab - upper_half * sin_tab, upper_half * cos_tab + lower_half * sin_tab], axis=-1)


def attend_local(q_rot, k_cache_out, v_cache_out, seq_lens):
    row_count, seq_len, kv_heads, _ = k_cache_out.shape
    q_heads = q_rot.shape[1]
    q_grouped = q_rot.reshape(row_count, kv_heads, q_heads // kv_heads, HEAD)
    scores = jnp.einsum("bkgd,bskd->bkgs", q_grouped, k_cache_out, preferred_element_type=jnp.float32) * HEAD ** -0.5
    visible = (jnp.arange(seq_len)[None, :] <= seq_lens[:, None])[:, None, None, :]
    scores = jnp.where(visible, scores, -jnp.inf)
    weights = jnp.exp(scores - jnp.max(scores, axis=-1, keepdims=True))
    weight_sum = jnp.sum(weights, axis=-1, keepdims=True)
    weighted = jnp.einsum("bkgs,bskd->bkgd", weights.astype(jnp.bfloat16), v_cache_out, preferred_element_type=jnp.float32)
    return (weighted / weight_sum).astype(jnp.bfloat16).reshape(row_count, q_heads * HEAD)


def solution(mesh):
    mx_size = mesh.shape["mx"]
    act_spec = P(None, "mx")
    cache_spec = P("mx", None, "my", None)
    in_specs = (act_spec, P("mx"), P("mx"), P("mx"), P("mx", "my"), P("my"), P("mx", "my"), P("my"), P("mx", "my"), P("my"), P("my", "mx"), P("mx", "my"), P("mx", "my"), P("my", "mx"), cache_spec, cache_spec)
    out_specs = (act_spec, cache_spec, cache_spec)

    def local_layer(x_in, seq_lens, gain_attn, gain_mlp, w_q, b_q, w_k, b_k, w_v, b_v, w_o, w_gate, w_up, w_down, k_cache, v_cache):
        hidden = x_in.shape[1] * mx_size
        x_f32 = x_in.astype(jnp.float32)
        attn_sq = lax.psum(jnp.sum(x_f32 * x_f32, axis=1, keepdims=True), "mx")
        normed = (x_f32 * lax.rsqrt(attn_sq / hidden + NORM_EPS) * gain_attn.astype(jnp.float32)).astype(jnp.bfloat16)
        q_cols = w_q.shape[1]
        kv_cols = w_k.shape[1]
        partials = jnp.concatenate([
            jnp.dot(normed, w_q, preferred_element_type=jnp.float32).astype(jnp.bfloat16),
            jnp.dot(normed, w_k, preferred_element_type=jnp.float32).astype(jnp.bfloat16),
            jnp.dot(normed, w_v, preferred_element_type=jnp.float32).astype(jnp.bfloat16),
        ], axis=1)
        projected = lax.psum_scatter(partials, "mx", scatter_dimension=0, tiled=True).astype(jnp.float32)
        row_count = projected.shape[0]
        kv_heads = kv_cols // HEAD
        q_vals = projected[:, :q_cols] + b_q.astype(jnp.float32)
        k_vals = projected[:, q_cols:q_cols + kv_cols] + b_k.astype(jnp.float32)
        v_vals = projected[:, q_cols + kv_cols:] + b_v.astype(jnp.float32)
        q_rot = apply_rotary(q_vals.reshape(row_count, q_cols // HEAD, HEAD), seq_lens).astype(jnp.bfloat16)
        k_rot = apply_rotary(k_vals.reshape(row_count, kv_heads, HEAD), seq_lens).astype(jnp.bfloat16)
        v_new = v_vals.reshape(row_count, kv_heads, HEAD).astype(jnp.bfloat16)
        at_slot = (jnp.arange(k_cache.shape[1])[None, :] == seq_lens[:, None])[:, :, None, None]
        k_cache_out = jnp.where(at_slot, k_rot[:, None], k_cache)
        v_cache_out = jnp.where(at_slot, v_new[:, None], v_cache)
        attn_rows = attend_local(q_rot, k_cache_out, v_cache_out, seq_lens)
        attn_all = lax.all_gather(attn_rows, "mx", axis=0, tiled=True)
        attn_proj = lax.psum(jnp.dot(attn_all, w_o, preferred_element_type=jnp.float32).astype(jnp.bfloat16), "my")
        x_mid = (x_f32 + attn_proj.astype(jnp.float32)).astype(jnp.bfloat16)
        mid_f32 = x_mid.astype(jnp.float32)
        mlp_sq = lax.psum(jnp.sum(mid_f32 * mid_f32, axis=1, keepdims=True), "mx")
        normed_mlp = (mid_f32 * lax.rsqrt(mlp_sq / hidden + NORM_EPS) * gain_mlp.astype(jnp.float32)).astype(jnp.bfloat16)
        ff_cols = w_gate.shape[1]
        gate_up = lax.psum(jnp.concatenate([
            jnp.dot(normed_mlp, w_gate, preferred_element_type=jnp.float32).astype(jnp.bfloat16),
            jnp.dot(normed_mlp, w_up, preferred_element_type=jnp.float32).astype(jnp.bfloat16),
        ], axis=1), "mx").astype(jnp.float32)
        hidden_act = (jax.nn.silu(gate_up[:, :ff_cols]) * gate_up[:, ff_cols:]).astype(jnp.bfloat16)
        down_proj = lax.psum(jnp.dot(hidden_act, w_down, preferred_element_type=jnp.float32).astype(jnp.bfloat16), "my")
        x_out = (mid_f32 + down_proj.astype(jnp.float32)).astype(jnp.bfloat16)
        return x_out, k_cache_out, v_cache_out

    return jax.shard_map(local_layer, mesh=mesh, in_specs=in_specs, out_specs=out_specs, check_vma=False)
```

profile of v0, /device:TPU:0, one launch (start us, length us, event | category | flops | bytes accessed | tf_op | source)
XLA Modules:
  0.0 245.2 jit_solution(8148330773259639867)
XLA Ops:
  7.2 0.0 copy-start
  7.2 0.0 reduce-scatter.2.cloned.1.call-start
  7.2 1.2 fusion.27
  8.4 15.4 %psum.35 = f32[64,1]{0,1:T(1,128)S(1)} all-reduce(f32[64,1]{0,1:T(1,128)S(1)} %bitcast.25), channel_id=1, replica_groups=mesh['my'=2,'mx'=8] {'mx'}, use_global_device_ids=true, to_apply=%region_1.0 | all-reduce | flops 64 | bytes 512 | tf_op jit(solution)/shard_map/psum | solution.py:45
  23.8 0.7 convert_element_type.97
  24.5 1.4 convolution_convert_fusion.5
  25.9 1.4 convolution_convert_fusion.4
  27.3 1.6 convolution_convert_fusion.2
  29.0 0.8 pad_maximum_fusion.1
  29.8 0.0 reduce-scatter.2.cloned.1.call-update
  29.8 0.0 all-reduce.4.cloned.1.call-start
  29.9 0.7 convert_element_type.104
  30.5 0.7 convert_element_type.105
  31.2 0.7 convert_element_type.107
  31.9 0.7 convert_element_type.103
  32.6 0.1 multiply_cosine_fusion
  32.7 0.7 iota_compare_fusion.1
  33.4 24.1 %reduce-scatter.2.cloned.1.call-done = bf16[8,3584]{1,0:T(8,128)(2,1)} async-done(((bf16[64,3584]{1,0:T(8,128)(2,1)}), bf16[8,3584]{1,0:T(8,128)(2,1)}) %reduce-scatter.2.cloned.1.call-update) | async-done | bytes 57360 | tf_op jit(solution)/shard_map/reduce_scatter | solution.py:54
  57.6 0.8 convert_element_type.102
  58.4 0.1 subtract_convert_fusion.1
  58.5 0.1 subtract_convert_fusion
  58.6 0.1 pad_maximum_fusion.2
  58.8 13.2 %broadcast_select_fusion.1 = (bf16[8,1024,4,128]{3,2,1,0:T(4,128)(2,1)S(1)}, bf16[8,1024,4,128]{3,2,1,0:T(4,128)(2,1)S(1)}) fusion(bf16[8,1024,4,128]{3,2,1,0:T(4,128)(2,1)} %param.30, pred[8,1024]{1,0:T(8,128)(4,1)S(1)} %get-tuple-element.16, bf16[8,4,128]{2,1,0:T(4,128)(2,1)S(1)} %copy.27, bf16[8,1024,4,128]{3,2,1,0:T(4,128)(2,1)} %param.31, ...), kind=kLoop, calls=%fused_computation.7 | loop fusion | flops 8388608 | bytes 33579008 | tf_op jit(solution)/shard_map/jit(_where)/select_n | solution.py:64
  71.9 0.0 copy-start.2
  71.9 0.0 copy-start.3
  71.9 3.4 %copy-done.2 = bf16[8,1024,4,128]{3,2,1,0:T(4,128)(2,1)} copy-done((bf16[8,1024,4,128]{3,2,1,0:T(4,128)(2,1)}, bf16[8,1024,4,128]{3,2,1,0:T(4,128)(2,1)S(1)}, u32[]{:S(2)}) %copy-start.2) | copy-done | bytes 8388632
  75.3 2.4 fusion.50
  77.7 0.3 fusion.23
  78.1 1.6 fusion.20
  79.7 0.1 reshape.146
  79.7 9.4 %all_gather.3 = bf16[64,2560]{1,0:T(8,128)(2,1)S(1)} all-gather(bf16[8,2560]{1,0:T(8,128)(2,1)S(1)} %reshape.146), channel_id=1, replica_groups=mesh['my'=2,'mx'=8] {'mx'}, dimensions={0}, use_global_device_ids=true | all-gather | bytes 368640 | tf_op jit(solution)/shard_map/all_gather | solution.py:67
  89.2 3.2 %convolution_convert_fusion.3 = bf16[64,640]{1,0:T(8,128)(2,1)} fusion(bf16[64,2560]{1,0:T(8,128)(2,1)S(1)} %all_gather.3, bf16[2560,640]{1,0:T(8,128)(2,1)} %param.26), kind=kOutput, calls=%fused_computation.17 | convolution fusion | flops 209756160 | bytes 3686400 | tf_op jit(solution)/shard_map/dot_general | solution.py:68
  92.4 0.0 all-reduce.4.cloned.1.call-update
  92.4 0.0 all-reduce.6.cloned.1.call-start
  92.5 17.3 %all-reduce.4.cloned.1.call-done = bf16[64,640]{1,0:T(8,128)(2,1)} async-done(((bf16[64,640]{1,0:T(8,128)(2,1)}), bf16[64,640]{1,0:T(8,128)(2,1)}) %all-reduce.4.cloned.1.call-update) | async-done | bytes 81936 | tf_op jit(solution)/shard_map/psum | solution.py:68
  109.8 1.0 fusion.31
  110.8 13.2 %psum.37 = f32[64,1]{0,1:T(1,128)S(1)} all-reduce(f32[64,1]{0,1:T(1,128)S(1)} %bitcast.24), channel_id=1, replica_groups=mesh['my'=2,'mx'=8] {'mx'}, use_global_device_ids=true, to_apply=%region_7.8 | all-reduce | flops 64 | bytes 512 | tf_op jit(solution)/shard_map/psum | solution.py:71
  124.0 9.3 %convolution_convert_fusion = bf16[64,13824]{1,0:T(8,128)(2,1)S(1)} fusion(bf16[640,13824]{1,0:T(8,128)(2,1)} %param.28, bf16[64,640]{1,0:T(8,128)(2,1)S(1)} %get-tuple-element.4, f32[640]{0:T(1024)S(1)} %convert_element_type.115, f32[64]{0:T(128)S(1)} %rsqrt_bitcast_fusion), kind=kOutput, calls=%fused_computation | convolution fusion | flops 1133510656 | bytes 19548928 | tf_op jit(solution)/shard_map/dot_general | solution.py:76
  133.3 9.3 %convolution_convert_fusion.1 = bf16[64,13824]{1,0:T(8,128)(2,1)S(1)} fusion(bf16[640,13824]{1,0:T(8,128)(2,1)} %param.27, bf16[64,640]{1,0:T(8,128)(2,1)S(1)} %get-tuple-element.4, f32[640]{0:T(1024)S(1)} %convert_element_type.115, f32[64]{0:T(128)S(1)} %rsqrt_bitcast_fusion), kind=kOutput, calls=%fused_computation.1 | convolution fusion | flops 1133510656 | bytes 19548928 | tf_op jit(solution)/shard_map/dot_general | solution.py:75
  142.6 2.0 pad_maximum_fusion
  144.7 0.0 all-reduce.6.cloned.1.call-update
  144.7 0.0 all-reduce.8.cloned.1.call-start
  144.7 64.0 %all-reduce.6.cloned.1.call-done = bf16[64,27648]{1,0:T(8,128)(2,1)} async-done(((bf16[64,27648]{1,0:T(8,128)(2,1)}), bf16[64,27648]{1,0:T(8,128)(2,1)}) %all-reduce.6.cloned.1.call-update) | async-done | bytes 3538960 | tf_op jit(solution)/shard_map/psum | solution.py:74
  208.7 2.5 %convert_element_type.119 = f32[64,27648]{1,0:T(8,128)S(1)} convert(bf16[64,27648]{1,0:T(8,128)(2,1)} %all-reduce.6.cloned.1.call-done) | non-fusion elementwise | flops 1769472 | bytes 10616832 | tf_op jit(solution)/shard_map/convert_element_type | solution.py:77
  211.2 8.5 %fusion.14 = bf16[64,640]{1,0:T(8,128)(2,1)} fusion(bf16[13824,640]{1,0:T(8,128)(2,1)} %param.29, f32[64,27648]{1,0:T(8,128)S(1)} %convert_element_type.119), kind=kOutput, calls=%fused_computation.16 | convolution fusion | flops 1137811456 | bytes 24854528 | tf_op jit(solution)/shard_map/dot_general | solution.py:79
  219.7 0.0 all-reduce.8.cloned.1.call-update
  219.7 17.4 %all-reduce.8.cloned.1.call-done = bf16[64,640]{1,0:T(8,128)(2,1)} async-done(((bf16[64,640]{1,0:T(8,128)(2,1)}), bf16[64,640]{1,0:T(8,128)(2,1)}) %all-reduce.8.cloned.1.call-update) | async-done | bytes 81936 | tf_op jit(solution)/shard_map/psum | solution.py:79
  237.2 1.5 fusion.34
  (18 shorter events, 0.1 us)
Async XLA Ops:
  7.2 20.2 %copy-start = (bf16[640,2560]{1,0:T(8,128)(2,1)S(1)}, bf16[640,2560]{1,0:T(8,128)(2,1)}, u32[]{:S(2)}) copy-start(bf16[640,2560]{1,0:T(8,128)(2,1)} %param.20) | copy-start | bytes 9830404
  7.2 50.4 %reduce-scatter.2.cloned.1.call-start = ((), (), s32[]{:S(2)}) async-start(), calls=%async_computation.1 | async-start | bytes 516096 | tf_op jit(solution)/shard_map/reduce_scatter | solution.py:54
  29.8 80.0 %all-reduce.4.cloned.1.call-start = ((), (), s32[]{:S(2)}) async-start(), calls=%async_computation.2 | async-start | bytes 163840 | tf_op jit(solution)/shard_map/psum | solution.py:68
  71.9 3.4 %copy-start.2 = (bf16[8,1024,4,128]{3,2,1,0:T(4,128)(2,1)}, bf16[8,1024,4,128]{3,2,1,0:T(4,128)(2,1)S(1)}, u32[]{:S(2)}) copy-start(bf16[8,1024,4,128]{3,2,1,0:T(4,128)(2,1)S(1)} %get-tuple-element.11) | copy-start | bytes 25165828
  71.9 6.2 %copy-start.3 = (bf16[8,1024,4,128]{3,2,1,0:T(4,128)(2,1)}, bf16[8,1024,4,128]{3,2,1,0:T(4,128)(2,1)S(1)}, u32[]{:S(2)}) copy-start(bf16[8,1024,4,128]{3,2,1,0:T(4,128)(2,1)S(1)} %get-tuple-element.12) | copy-start | bytes 25165828
  78.1 14.4 %copy-start.5 = (bf16[640]{0:T(1024)(128)(2,1)S(1)}, bf16[640]{0:T(1024)(128)(2,1)}, u32[]{:S(2)}) copy-start(bf16[640]{0:T(1024)(128)(2,1)} %param.19) | copy-start | bytes 3844
  78.1 31.7 %copy-start.4 = (bf16[64,640]{1,0:T(8,128)(2,1)S(1)}, bf16[64,640]{1,0:T(8,128)(2,1)}, u32[]{:S(2)}) copy-start(bf16[64,640]{1,0:T(8,128)(2,1)} %param.16) | copy-start | bytes 245764
  92.4 116.3 %all-reduce.6.cloned.1.call-start = ((), (), s32[]{:S(2)}) async-start(), calls=%async_computation.3 | async-start | bytes 7077888 | tf_op jit(solution)/shard_map/psum | solution.py:74
  144.7 92.5 %all-reduce.8.cloned.1.call-start = ((), (), s32[]{:S(2)}) async-start(), calls=%async_computation.4 | async-start | bytes 163840 | tf_op jit(solution)/shard_map/psum | solution.py:79
  211.2 27.5 %copy-start.1 = (bf16[640,2560]{1,0:T(8,128)(2,1)S(1)}, bf16[640,2560]{1,0:T(8,128)(2,1)}, u32[]{:S(2)}) copy-start(bf16[640,2560]{1,0:T(8,128)(2,1)} %param.20) | copy-start | bytes 9830404
Sparse Core Ops, SparseCore 0:
  29.9 27.6 reduce-scatter.1
  92.5 17.1 all-reduce.3
  144.8 63.8 all-reduce.5
  219.8 17.2 all-reduce.7
where the time goes:
time: 246 us; the launch traced here: 245 us
  waiting for transfers between devices  123 us (50%)
  matrix products  38.8 us (16%)
  blocking collectives  38 us (15%)
  other arithmetic  27.9 us (11%)
  between operations  14 us (6%)
  local copies, waits for them, and re-layouts  3.53 us (1%)
    psum x1, waiting for transfers between devices, local_layer(): lax.psum(jnp.concatenate([jnp.dot(normed_mlp, w_gate, preferred_element_t...  64 us
    reduce_scatter x1, waiting for transfers between devices, local_layer(): lax.psum_scatter(partials, 'mx', scatter_dimension=0, tiled=True)  24.1 us
    psum x1, waiting for transfers between devices, local_layer(): lax.psum(jnp.dot(hidden_act, w_down, preferred_element_type=jnp.float32)....  17.4 us
    psum x1, waiting for transfers between devices, local_layer(): lax.psum(jnp.dot(attn_all, w_o, preferred_element_type=jnp.float32).astyp...  17.3 us
    psum x1, blocking collectives, local_layer(): attn_sq = lax.psum(jnp.sum(x_f32 * x_f32, axis=1, keepdims=True), 'mx')  15.4 us
    psum x1, blocking collectives, local_layer(): mlp_sq = lax.psum(jnp.sum(mid_f32 * mid_f32, axis=1, keepdims=True), 'mx')  13.2 us
    select_n x1, other arithmetic, local_layer(): k_cache_out = jnp.where(at_slot, k_rot[:, None], k_cache)  13.2 us
    all_gather x1, blocking collectives, local_layer(): attn_all = lax.all_gather(attn_rows, 'mx', axis=0, tiled=True)  9.4 us
  transfers between devices with their start and end apart: 4, of which 4 were waited for; matrix products, arithmetic and copies ran while one was open for 1% of the time, Pallas kernels for 0%

commit v1 on v0

v1 whole, which is shorter than its diff:
```python
import functools

import jax
import jax.numpy as jnp
from jax import lax
from jax.experimental import pallas as pl
from jax.experimental.pallas import tpu as pltpu
from jax.sharding import PartitionSpec as P

HEAD = 128
NORM_EPS = 1e-6
ROPE_THETA = 1000000.0
MESH = pl.DeviceIdType.MESH
F32 = jnp.float32
BF16 = jnp.bfloat16
VMEM = pltpu.VMEM
DMA = pltpu.SemaphoreType.DMA


def neighbours(mx):
    core = lax.rem(mx, 2)
    chip = mx // 2
    x_pos = lax.rem(chip, 2)
    y_pos = chip // 2
    others = (y_pos * 2 + (1 - x_pos), (1 - y_pos) * 2 + x_pos, (1 - y_pos) * 2 + (1 - x_pos))
    return core, chip, chip * 2 + (1 - core), others


def send(src, dst, send_sem, recv_sem, my, mx):
    copy = pltpu.make_async_remote_copy(src_ref=src, dst_ref=dst, send_sem=send_sem, recv_sem=recv_sem, device_id=(my, mx), device_id_type=MESH)
    copy.start()
    return copy


def drain(ref, sem):
    pltpu.make_async_copy(ref, ref, sem).wait()


def share_stat(square_sum, my, mx, stat_out, stat_in, send_sems, recv_sems):
    rows = square_sum.shape[0]
    turned = jnp.transpose(jnp.broadcast_to(square_sum, (rows, 128)))[0:8]
    stat_out[...] = turned
    copies = []
    for step in range(1, 8):
        peer = lax.rem(mx + step, 8)
        copies.append(send(stat_out, stat_in.at[mx], send_sems.at[step], recv_sems.at[step], my, peer))
    stat_in[mx] = turned
    for copy in copies:
        copy.wait()
    total = jnp.sum(stat_in[...], axis=0)
    return jnp.transpose(jnp.broadcast_to(total[0:1], (128, rows)))[:, 0:1]


def enter(my, mx, with_z):
    barrier = pltpu.get_barrier_semaphore()
    for step in range(1, 8):
        pl.semaphore_signal(barrier, inc=1, device_id=(my, lax.rem(mx + step, 8)), device_id_type=MESH)
    if with_z:
        pl.semaphore_signal(barrier, inc=1, device_id=(1 - my, mx), device_id_type=MESH)
    pl.semaphore_wait(barrier, 8 if with_z else 7)


def qkv_kernel(hidden, pieces, x_ref, gain_ref, wq_hbm, wk_hbm, wv_hbm, out_ref, wq_v, wk_v, wv_v, part, pair_in, chip_in, stat_out, stat_in,
               w_sems, stat_send, stat_recv, pair_send, pair_recv, chip_send, chip_recv):
    my = lax.axis_index("my")
    mx = lax.axis_index("mx")
    core, chip, partner, others = neighbours(mx)
    loads = [pltpu.make_async_copy(src, dst, w_sems.at[n]) for n, (src, dst) in enumerate(((wq_hbm, wq_v), (wk_hbm, wk_v), (wv_hbm, wv_v)))]
    for load in loads:
        load.start()
    enter(my, mx, False)
    x = x_ref[...].astype(F32)
    stat = share_stat(jnp.sum(x * x, axis=1, keepdims=True), my, mx, stat_out, stat_in, stat_send, stat_recv)
    normed = (x * lax.rsqrt(stat / hidden + NORM_EPS) * gain_ref[...].astype(F32)).astype(BF16)
    weights = (wq_v, wk_v, wv_v)
    copies = []
    waited = set()
    pair_copies = []
    for n, (which, first, width, out_first) in enumerate(pieces):
        if which not in waited:
            loads[which].wait()
            waited.add(which)
        cols = pl.ds(out_first, width)
        product = jnp.dot(normed, weights[which][:, first:first + width], preferred_element_type=F32)
        part[:, :, :, cols] = product.reshape(4, 2, 8, width).astype(BF16)
        pair_copies.append(send(part.at[:, 1 - core, :, cols], pair_in.at[:, :, cols], pair_send.at[n], pair_recv.at[n], my, partner))
    for n, (which, first, width, out_first) in enumerate(pieces):
        cols = pl.ds(out_first, width)
        pair_copies[n].wait_recv()
        pair_in[:, :, cols] = (part[:, core, :, cols].astype(F32) + pair_in[:, :, cols].astype(F32)).astype(BF16)
        for k, other in enumerate(others):
            copies.append(send(pair_in.at[other, :, cols], chip_in.at[k, :, cols], chip_send.at[n, k], chip_recv.at[n, k], my, other * 2 + core))
    for n, (which, first, width, out_first) in enumerate(pieces):
        cols = pl.ds(out_first, width)
        total = pair_in[chip, :, cols].astype(F32)
        for k in range(3):
            copies[n * 3 + k].wait_recv()
            total = total + chip_in[k, :, cols].astype(F32)
        out_ref[:, cols] = total
    for copy in pair_copies + copies:
        copy.wait_send()


def attend_kernel(lens_ref, proj_ref, bq_ref, bk_ref, bv_ref, cos_ref, sin_ref, k_hbm, v_hbm, ko_hbm, vo_hbm, attn_ref,
                  k_buf, v_buf, q_s, k_s, v_s, o_s, in_sems, out_sems):
    rows, slots, _ = k_buf.shape
    kv_heads = bk_ref.shape[0] // HEAD
    heads = bq_ref.shape[0] // HEAD
    group = heads // kv_heads
    q_cols = heads * HEAD
    kv_cols = kv_heads * HEAD
    for b in range(rows):
        pltpu.make_async_copy(k_hbm.at[b], k_buf.at[b], in_sems.at[0, b]).start()
        pltpu.make_async_copy(v_hbm.at[b], v_buf.at[b], in_sems.at[1, b]).start()
    cos = cos_ref[...]
    sin = sin_ref[...]
    q_s[...] = jnp.zeros_like(q_s)

    def biased(first, bias_ref, h):
        return proj_ref[:, first + h * HEAD:first + (h + 1) * HEAD] + bias_ref[h * HEAD:(h + 1) * HEAD].astype(F32)[None, :]

    def rotated(vals):
        return vals * cos + pltpu.roll(vals, HEAD // 2, 1) * sin

    for h in range(heads):
        q_s[:, h, :] = rotated(biased(0, bq_ref, h))
    for h in range(kv_heads):
        k_new = rotated(biased(q_cols, bk_ref, h))
        v_new = biased(q_cols + kv_cols, bv_ref, h)
        for r in range(16 // kv_heads):
            k_s[:, r * kv_heads + h, :] = k_new
            v_s[:, r * kv_heads + h, :] = v_new
    q_pad = q_s.shape[1]
    per_tile = 16 // kv_heads
    sub = lax.broadcasted_iota(jnp.int32, (16, HEAD), 0) // kv_heads
    col = lax.broadcasted_iota(jnp.int32, (q_pad, slots), 1)
    row = lax.broadcasted_iota(jnp.int32, (q_pad, slots), 0)
    row_head = sum((row >= group * n).astype(jnp.int32) for n in range(1, kv_heads))
    own_head = lax.rem(col, kv_heads) == row_head

    @pl.loop(0, rows)
    def _(b):
        position = lens_ref[b]
        base = pl.multiple_of(position // per_tile * 16, 16)
        at_slot = sub == lax.rem(position, per_tile)
        for buf, new, hbm, n in ((k_buf, k_s, k_hbm, 0), (v_buf, v_s, v_hbm, 1)):
            pltpu.make_async_copy(hbm.at[b], buf.at[b], in_sems.at[n, b]).wait()
            window = buf[b, pl.ds(base, 16), :].astype(F32)
            buf[b, pl.ds(base, 16), :] = jnp.where(at_slot, new[b], window).astype(BF16)
        scores = lax.dot_general(q_s[b].astype(BF16), k_buf[b], (((1,), (1,)), ((), ())), preferred_element_type=F32) * HEAD ** -0.5
        scores = jnp.where(own_head & (col < (position + 1) * kv_heads), scores, -jnp.inf)
        top = jnp.max(scores, axis=1, keepdims=True)
        top = jnp.where(top == -jnp.inf, 0.0, top)
        weights = jnp.exp(scores - top)
        weight_sum = jnp.sum(weights, axis=1, keepdims=True)
        weighted = jnp.dot(weights.astype(BF16), v_buf[b], preferred_element_type=F32)
        o_s[b] = weighted / weight_sum
        pltpu.make_async_copy(k_buf.at[b], ko_hbm.at[b], out_sems.at[0, b]).start()
        pltpu.make_async_copy(v_buf.at[b], vo_hbm.at[b], out_sems.at[1, b]).start()

    for h in range(heads):
        attn_ref[:, h * HEAD:(h + 1) * HEAD] = o_s[:, h, :].astype(BF16)
    for b in range(rows):
        pltpu.make_async_copy(k_buf.at[b], ko_hbm.at[b], out_sems.at[0, b]).wait()
        pltpu.make_async_copy(v_buf.at[b], vo_hbm.at[b], out_sems.at[1, b]).wait()


def mlp_kernel(hidden, chunks, per_load, attn_ref, x_ref, gain_ref, wo_hbm, wg_hbm, wu_hbm, wd_hbm, out_ref,
               attn_all, wo_v, wg_v, wu_v, wd_v, z_out, z_in, stat_out, stat_in, h_v, m_v, acc, mine, theirs, pair_in, chip_in, act,
               wo_sem, wg_sems, wu_sems, wd_sems, ag_send, ag_recv, z_send, z_recv, stat_send, stat_recv,
               pair_send, pair_recv, chip_send, chip_recv, act_send, act_recv, fwd_send, fwd_recv):
    my = lax.axis_index("my")
    mx = lax.axis_index("mx")
    core, chip, partner, others = neighbours(mx)
    half = act.shape[4]
    loads = chunks // per_load
    load_cols = per_load * 2 * half

    load_wo = pltpu.make_async_copy(wo_hbm, wo_v, wo_sem)
    load_wo.start()

    def load_gate(n):
        cols = pl.ds(pl.multiple_of(n * load_cols, 128), load_cols)
        return pltpu.make_async_copy(wg_hbm.at[:, cols], wg_v.at[n], wg_sems.at[n]), pltpu.make_async_copy(wu_hbm.at[:, cols], wu_v.at[n], wu_sems.at[n])

    def load_down(n):
        span = pl.ds(n * per_load, per_load)
        return pltpu.make_async_copy(wd_hbm.at[span], wd_v.at[span], wd_sems.at[n])

    @pl.loop(0, loads)
    def _(n):
        for load in load_gate(n):
            load.start()

    @pl.loop(0, loads)
    def _(n):
        load_down(n).start()

    enter(my, mx, True)

    copies = []
    for step in range(1, 8):
        peer = lax.rem(mx + step, 8)
        copies.append(send(attn_ref, attn_all.at[mx], ag_send.at[step], ag_recv.at[step], my, peer))
    attn_all[mx] = attn_ref[...]
    load_wo.wait()
    for copy in copies:
        copy.wait()
    rows = x_ref.shape[0]
    attn = attn_all[...].reshape(rows, attn_ref.shape[1])
    z_out[0] = jnp.dot(attn, wo_v[...], preferred_element_type=F32).astype(BF16)
    z_copy = send(z_out.at[0], z_in.at[0], z_send.at[0], z_recv.at[0], 1 - my, mx)
    z_copy.wait()
    mid = (x_ref[...].astype(F32) + (z_out[0].astype(F32) + z_in[0].astype(F32))).astype(BF16)
    m_v[...] = mid
    mid = mid.astype(F32)
    stat = share_stat(jnp.sum(mid * mid, axis=1, keepdims=True), my, mx, stat_out, stat_in, stat_send, stat_recv)
    h_v[...] = (mid * lax.rsqrt(stat / hidden + NORM_EPS) * gain_ref[...].astype(F32)).astype(BF16)
    acc[...] = jnp.zeros_like(acc)

    def products(k, part, dest):
        n = k // per_load
        cols = pl.ds(pl.multiple_of(lax.rem(k, per_load) * (2 * half) + part * half, 128), half)
        h = h_v[...]
        for which, weights in ((0, wg_v), (1, wu_v)):
            out = jnp.dot(h, weights[n, :, cols], preferred_element_type=F32)
            dest[k, :, which] = out.astype(BF16).reshape(4, 16, half)

    def multiply(k):
        @pl.when(lax.rem(k, per_load) == 0)
        def _():
            for load in load_gate(k // per_load):
                load.wait()

        products(k, 1 - core, theirs)
        send(theirs.at[k], pair_in.at[k], pair_send.at[k], pair_recv.at[k], my, partner)
        products(k, core, mine)

    def scatter(k):
        drain(pair_in.at[k], pair_recv.at[k])
        pair_in[k] = (mine[k].astype(F32) + pair_in[k].astype(F32)).astype(BF16)
        for n, other in enumerate(others):
            send(pair_in.at[k, other], chip_in.at[k, n], chip_send.at[k], chip_recv.at[k], my, other * 2 + core)

    def activate(k):
        drain(chip_in.at[k], chip_recv.at[k])
        total = pair_in[k, chip].astype(F32)
        for n in range(3):
            total = total + chip_in[k, n].astype(F32)
        gate = total[0]
        act[k, core, chip] = (gate * jax.nn.sigmoid(gate) * total[1]).astype(BF16)
        mine_act = act.at[k, core, chip]
        for other in others:
            send(mine_act, mine_act, act_send.at[k], act_recv.at[k], my, other * 2 + core)
        send(mine_act, mine_act, fwd_send.at[k], fwd_recv.at[k], my, partner)

    def forward(k):
        drain(act.at[k, core, pl.ds(0, 3)], act_recv.at[k])
        for other in others:
            block = act.at[k, core, other]
            send(block, block, fwd_send.at[k], fwd_recv.at[k], my, partner)

    def contract(k):
        @pl.when(lax.rem(k, per_load) == 0)
        def _():
            load_down(k // per_load).wait()

        drain(act.at[k, 1 - core], fwd_recv.at[k])
        total = acc[...]
        for part in range(2):
            total = total + jnp.dot(act[k, part].reshape(rows, half), wd_v[k, part], preferred_element_type=F32)
        acc[...] = total

    stages = ((contract, 10), (forward, 8), (activate, 5), (scatter, 2), (multiply, 0))

    @pl.loop(0, chunks + stages[0][1])
    def _(t):
        for stage, lag in stages:
            @pl.when(jnp.logical_and(t >= lag, t < chunks + lag))
            def _():
                stage(t - lag)

    z_out[1] = acc[...].astype(BF16)
    z_copy = send(z_out.at[1], z_in.at[1], z_send.at[1], z_recv.at[1], 1 - my, mx)
    z_copy.wait()
    out_ref[...] = (m_v[...].astype(F32) + (z_out[1].astype(F32) + z_in[1].astype(F32))).astype(BF16)

    @pl.loop(0, chunks)
    def _(k):
        drain(theirs.at[k], pair_send.at[k])
        drain(chip_in.at[k], chip_send.at[k])
        drain(act.at[k, core, pl.ds(0, 3)], act_send.at[k])
        drain(act.at[k, core], fwd_send.at[k])


def solution(mesh):
    mx_size = mesh.shape["mx"]
    act_spec = P(None, "mx")
    cache_spec = P("mx", None, "my", None)
    in_specs = (act_spec, P("mx"), P("mx"), P("mx"), P("mx", "my"), P("my"), P("mx", "my"), P("my"), P("mx", "my"), P("my"), P("my", "mx"), P("mx", "my"), P("mx", "my"), P("my", "mx"), cache_spec, cache_spec)
    out_specs = (act_spec, cache_spec, cache_spec)
    vmem = pl.BlockSpec(memory_space=pltpu.VMEM)
    smem = pl.BlockSpec(memory_space=pltpu.SMEM)
    anywhere = pl.BlockSpec(memory_space=pl.ANY)

    def local_layer(x_in, seq_lens, gain_attn, gain_mlp, w_q, b_q, w_k, b_k, w_v, b_v, w_o, w_gate, w_up, w_down, k_cache, v_cache):
        rows, cols = x_in.shape
        hidden = cols * mx_size
        q_cols = w_q.shape[1]
        kv_cols = w_k.shape[1]
        heads = q_cols // HEAD
        kv_heads = kv_cols // HEAD
        local_rows = rows // mx_size
        qkv_cols = q_cols + 2 * kv_cols
        pieces = ((0, 0, q_cols // 2, 0), (0, q_cols // 2, q_cols // 2, q_cols // 2), (1, 0, kv_cols, q_cols), (2, 0, kv_cols, q_cols + kv_cols))

        inv_freq = ROPE_THETA ** (-2.0 * jnp.arange(HEAD // 2, dtype=F32) / HEAD)
        angles = seq_lens.astype(F32)[:, None] * inv_freq
        cos_half = jnp.cos(angles)
        sin_half = jnp.sin(angles)
        cos_tab = jnp.concatenate([cos_half, cos_half], axis=1)
        sin_tab = jnp.concatenate([-sin_half, sin_half], axis=1)

        projected = pl.pallas_call(
            functools.partial(qkv_kernel, hidden, pieces),
            name="qkv",
            out_shape=jax.ShapeDtypeStruct((local_rows, qkv_cols), F32),
            in_specs=[vmem, vmem, anywhere, anywhere, anywhere],
            out_specs=vmem,
            scratch_shapes=[
                VMEM(w_q.shape, BF16), VMEM(w_k.shape, BF16), VMEM(w_v.shape, BF16),
                VMEM((4, 2, local_rows, qkv_cols), BF16), VMEM((4, local_rows, qkv_cols), BF16), VMEM((3, local_rows, qkv_cols), BF16),
                VMEM((8, rows), F32), VMEM((8, 8, rows), F32),
                DMA((3,)), DMA((8,)), DMA((8,)), DMA((4,)), DMA((4,)), DMA((4, 3)), DMA((4, 3)),
            ],
            compiler_params=pltpu.CompilerParams(collective_id=0, has_side_effects=True, vmem_limit_bytes=16 * 2 ** 20),
        )(x_in, gain_attn.reshape(1, cols), w_q, w_k, w_v)

        slots = k_cache.shape[1] * kv_heads
        flat = (local_rows, slots, HEAD)
        padded = (heads + 7) // 8 * 8
        k_flat, v_flat, attn = pl.pallas_call(
            attend_kernel,
            name="attend",
            out_shape=(jax.ShapeDtypeStruct(flat, BF16), jax.ShapeDtypeStruct(flat, BF16), jax.ShapeDtypeStruct((local_rows, q_cols), BF16)),
            in_specs=[smem, vmem, vmem, vmem, vmem, vmem, vmem, anywhere, anywhere],
            out_specs=(anywhere, anywhere, vmem),
            scratch_shapes=[
                VMEM(flat, BF16), VMEM(flat, BF16),
                VMEM((local_rows, padded, HEAD), F32), VMEM((local_rows, 16, HEAD), F32), VMEM((local_rows, 16, HEAD), F32), VMEM((local_rows, padded, HEAD), F32),
                DMA((2, local_rows)), DMA((2, local_rows)),
            ],
            compiler_params=pltpu.CompilerParams(vmem_limit_bytes=40 * 2 ** 20),
        )(seq_lens, projected, b_q, b_k, b_v, cos_tab, sin_tab, k_cache.reshape(flat), v_cache.reshape(flat))

        ff_cols = w_gate.shape[1]
        half = 256
        chunks = ff_cols // (2 * half)
        per_load = 3
        loads = chunks // per_load
        x_out = pl.pallas_call(
            functools.partial(mlp_kernel, hidden, chunks, per_load),
            name="mlp",
            out_shape=jax.ShapeDtypeStruct((rows, cols), BF16),
            in_specs=[vmem, vmem, vmem, anywhere, anywhere, anywhere, anywhere],
            out_specs=vmem,
            scratch_shapes=[
                VMEM((8, local_rows, q_cols), BF16), VMEM(w_o.shape, BF16),
                VMEM((loads, cols, per_load * 2 * half), BF16), VMEM((loads, cols, per_load * 2 * half), BF16), VMEM((chunks, 2, half, cols), BF16),
                VMEM((2, rows, cols), BF16), VMEM((2, rows, cols), BF16), VMEM((8, rows), F32), VMEM((8, 8, rows), F32),
                VMEM((rows, cols), BF16), VMEM((rows, cols), BF16), VMEM((rows, cols), F32),
                VMEM((chunks, 4, 2, 16, half), BF16), VMEM((chunks, 4, 2, 16, half), BF16), VMEM((chunks, 4, 2, 16, half), BF16),
                VMEM((chunks, 3, 2, 16, half), BF16), VMEM((chunks, 2, 4, 16, half), BF16),
                DMA, DMA((loads,)), DMA((loads,)), DMA((loads,)), DMA((8,)), DMA((8,)), DMA((2,)), DMA((2,)), DMA((8,)), DMA((8,)),
                DMA((chunks,)), DMA((chunks,)), DMA((chunks,)), DMA((chunks,)), DMA((chunks,)), DMA((chunks,)), DMA((chunks,)), DMA((chunks,)),
            ],
            compiler_params=pltpu.CompilerParams(collective_id=1, has_side_effects=True, vmem_limit_bytes=67043328),
        )(attn, x_in, gain_mlp.reshape(1, cols), w_o, w_gate, w_up, w_down.reshape(chunks, 2, half, cols))
        return x_out, k_flat.reshape(k_cache.shape), v_flat.reshape(v_cache.shape)

    return jax.shard_map(local_layer, mesh=mesh, in_specs=in_specs, out_specs=out_specs, check_vma=False)
```

time: 246 us -> 105 us (0.43)
  waiting for transfers between devices: 123 us -> 0 us
  Pallas kernels: 0 us -> 88.5 us
  matrix products: 38.8 us -> 0 us
  blocking collectives: 38 us -> 0 us
  other arithmetic: 27.9 us -> 0.86 us
  between operations: 14 us -> 0.69 us
  local copies, waits for them, and re-layouts: 3.53 us -> 14.5 us
    psum x3 -> x0, waiting for transfers between devices: 98.7 us -> none  [the longest x1 64 us: local_layer(): lax.psum(jnp.concatenate([jnp.dot(normed_mlp, w_gate, preferred_element_t...]
    pallas_call x0 -> x3, Pallas kernels: none -> 88.5 us  [the longest x1 63.8 us: local_layer(): pl.pallas_call(functools.partial(mlp_kernel, hidden, chunks, per_load), n...]
    dot_general x9 -> x0, matrix products: 38.8 us -> none  [the longest x1 9.32 us: local_layer(): jnp.dot(normed_mlp, w_up, preferred_element_type=jnp.float32)]
    psum x2 -> x0, blocking collectives: 28.6 us -> none  [the longest x1 15.4 us: local_layer(): attn_sq = lax.psum(jnp.sum(x_f32 * x_f32, axis=1, keepdims=True), 'mx')]
    reduce_scatter x1 -> x0, waiting for transfers between devices: 24.1 us -> none  [local_layer(): lax.psum_scatter(partials, 'mx', scatter_dimension=0, tiled=True)]
    select_n x1 -> x0, other arithmetic: 13.2 us -> none  [local_layer(): k_cache_out = jnp.where(at_slot, k_rot[:, None], k_cache)]
    unnamed x12 -> x23, local copies, waits for them, and re-layouts: 3.41 us -> 13.2 us
    all_gather x1 -> x0, blocking collectives: 9.4 us -> none  [local_layer(): attn_all = lax.all_gather(attn_rows, 'mx', axis=0, tiled=True)]
  transfers between devices with their start and end apart: 4 -> 0, of which waited for: 4 -> 0; matrix products, arithmetic and copies ran while one was open for 1% -> 0% of each run, Pallas kernels for 0% -> 0%
where the time goes in v1:
time: 105 us
  Pallas kernels  88.5 us (84%)
  local copies, waits for them, and re-layouts  14.5 us (14%)
    pallas_call x1, Pallas kernels, local_layer(): pl.pallas_call(functools.partial(mlp_kernel, hidden, chunks, per_load), n...  63.8 us
    pallas_call x1, Pallas kernels, local_layer(): pl.pallas_call(functools.partial(qkv_kernel, hidden, pieces), name='qkv',...  15.4 us
    unnamed x23, local copies, waits for them, and re-layouts  13.2 us
    pallas_call x1, Pallas kernels, local_layer(): pl.pallas_call(attend_kernel, name='attend', out_shape=(jax.ShapeDtypeStr...  9.33 us

profile of v1, /device:TPU:0, one launch (start us, length us, event | category | flops | bytes accessed | tf_op | source)
XLA Modules:
  0.0 104.6 jit_solution(2537757203933633507)
XLA Ops:
  0.6 0.7 convert_element_type.3
  1.3 0.1 fusion
  1.4 0.1 pad_maximum_fusion
  1.5 0.7 reshape.33.gain_ref
  2.2 0.0 copy-start.1
  2.2 1.9 %copy-done.1 = bf16[640,2560]{1,0:T(8,128)(2,1)S(1)} copy-done((bf16[640,2560]{1,0:T(8,128)(2,1)S(1)}, bf16[640,2560]{1,0:T(8,128)(2,1)}, u32[]{:S(2)}) %copy-start.1) | copy-done | bytes 3276824
  4.1 0.0 copy-start.2
  4.1 1.1 %copy-done.2 = bf16[640,512]{1,0:T(8,128)(2,1)S(1)} copy-done((bf16[640,512]{1,0:T(8,128)(2,1)S(1)}, bf16[640,512]{1,0:T(8,128)(2,1)}, u32[]{:S(2)}) %copy-start.2) | copy-done | bytes 655384
  5.2 0.0 copy-start.3
  5.2 1.1 %copy-done.3 = bf16[640,512]{1,0:T(8,128)(2,1)S(1)} copy-done((bf16[640,512]{1,0:T(8,128)(2,1)S(1)}, bf16[640,512]{1,0:T(8,128)(2,1)}, u32[]{:S(2)}) %copy-start.3) | copy-done | bytes 655384
  6.3 0.0 copy-start.4
  6.3 0.9 copy-done.4
  7.2 15.4 %qkv.1.proj_ref = f32[8,3584]{1,0:T(8,128)S(1)} custom-call(bf16[64,640]{1,0:T(8,128)(2,1)S(1)} %copy-done.4, bf16[1,640]{1,0:T(2,128)(2,1)S(1)} %reshape.33.gain_ref, bf16[640,2560]{1,0:T(8,128)(2,1)S(1)} %copy-done.1, bf16[640,512]{1,0:T(8,128)(2,1)S(1)} %copy-done.2, bf16[640,512]{1,0:T(8,128)(2,1)S(1)} %copy-done.3), custom_call_target="tpu_custom_call" | custom-call | tf_op jit(solution)/shard_map/qkv/pallas_call | solution.py:324
  22.6 0.0 copy-start
  22.6 3.4 %copy-done = bf16[8,1024,4,128]{3,2,1,0:T(4,128)(2,1)S(1)} copy-done((bf16[8,1024,4,128]{3,2,1,0:T(4,128)(2,1)S(1)}, bf16[8,1024,4,128]{3,2,1,0:T(4,128)(2,1)}, u32[]{:S(2)}) %copy-start) | copy-done | bytes 8388632
  26.0 0.0 copy-start.6
  26.0 0.7 copy-done.6
  26.7 0.0 copy-start.7
  26.7 0.7 copy-done.7
  27.4 0.0 copy-start.8
  27.4 0.7 copy-done.8
  28.1 0.0 copy-start.9
  28.1 0.7 copy-done.9
  28.7 0.0 copy-start.10
  28.7 9.3 %attend.1 = (bf16[8,4096,128]{2,1,0:T(8,128)(2,1)}, bf16[8,4096,128]{2,1,0:T(8,128)(2,1)}, bf16[8,2560]{1,0:T(8,128)(2,1)S(1)}) custom-call(s32[8]{0:T(128)S(1)} %copy-done.9, f32[8,3584]{1,0:T(8,128)S(1)} %qkv.1.proj_ref, bf16[2560]{0:T(1024)(128)(2,1)S(1)} %copy-done.6, bf16[512]{0:T(512)(128)(2,1)S(1)} %copy-done.7, bf16[512]{0:T(512)(128)(2,1)S(1)} %copy-done.8, ...), custom_call_target="tpu_custom_call" | custom-call | tf_op jit(solution)/shard_map/attend/pallas_call | solution.py:342
  38.0 0.0 copy-start.5
  38.1 0.6 copy-done.5
  38.7 0.0 copy-done.10
  38.7 0.6 reshape.36.gain_ref
  39.3 63.8 %mlp.1 = bf16[64,640]{1,0:T(8,128)(2,1)} custom-call(bf16[8,2560]{1,0:T(8,128)(2,1)} %copy-done.5, bf16[64,640]{1,0:T(8,128)(2,1)} %x_ref.3, bf16[1,640]{1,0:T(2,128)(2,1)} %reshape.36.gain_ref, bf16[2560,640]{1,0:T(8,128)(2,1)} %wo_hbm.1, bf16[640,13824]{1,0:T(8,128)(2,1)} %wg_hbm.1, bf16[640,13824]{1,0:T(8,128)(2,1)} %wu_hbm.1, ...), custom_call_target="tpu_custom_call" | custom-call | tf_op jit(solution)/shard_map/mlp/pallas_call | solution.py:361
  103.0 1.5 %copy.20 = bf16[64,640]{1,0:T(8,128)(2,1)} copy(bf16[64,640]{1,0:T(8,128)(2,1)} %mlp.1) | data formatting | bytes 163840
  (1 shorter events, 0.0 us)
Async XLA Ops:
  2.2 1.9 %copy-start.1 = (bf16[640,2560]{1,0:T(8,128)(2,1)S(1)}, bf16[640,2560]{1,0:T(8,128)(2,1)}, u32[]{:S(2)}) copy-start(bf16[640,2560]{1,0:T(8,128)(2,1)} %wq_hbm.1) | copy-start | bytes 9830404
  4.1 1.1 %copy-start.2 = (bf16[640,512]{1,0:T(8,128)(2,1)S(1)}, bf16[640,512]{1,0:T(8,128)(2,1)}, u32[]{:S(2)}) copy-start(bf16[640,512]{1,0:T(8,128)(2,1)} %wk_hbm.1) | copy-start | bytes 1966084
  5.2 1.1 %copy-start.3 = (bf16[640,512]{1,0:T(8,128)(2,1)S(1)}, bf16[640,512]{1,0:T(8,128)(2,1)}, u32[]{:S(2)}) copy-start(bf16[640,512]{1,0:T(8,128)(2,1)} %wv_hbm.1) | copy-start | bytes 1966084
  6.3 0.9 copy-start.4
  22.6 3.4 %copy-start = (bf16[8,1024,4,128]{3,2,1,0:T(4,128)(2,1)S(1)}, bf16[8,1024,4,128]{3,2,1,0:T(4,128)(2,1)}, u32[]{:S(2)}) copy-start(bf16[8,1024,4,128]{3,2,1,0:T(4,128)(2,1)} %param.30) | copy-start | bytes 25165828
  26.0 0.7 copy-start.6
  26.7 0.7 copy-start.7
  27.4 0.7 copy-start.8
  28.1 0.7 copy-start.9
  28.7 10.0 %copy-start.10 = (bf16[640]{0:T(1024)(128)(2,1)S(1)}, bf16[640]{0:T(1024)(128)(2,1)}, u32[]{:S(2)}) copy-start(bf16[640]{0:T(1024)(128)(2,1)} %param.19) | copy-start | bytes 3844
  38.0 0.6 copy-start.5

commit v2 on v1

v2 whole, which is shorter than its diff:
```python
import functools

import jax
import jax.numpy as jnp
from jax import lax
from jax.experimental import pallas as pl
from jax.experimental.pallas import tpu as pltpu
from jax.sharding import PartitionSpec as P

HEAD = 128
NORM_EPS = 1e-6
ROPE_THETA = 1000000.0
MESH = pl.DeviceIdType.MESH
F32 = jnp.float32
BF16 = jnp.bfloat16
VMEM = pltpu.VMEM
DMA = pltpu.SemaphoreType.DMA


def neighbours(mx):
    core = lax.rem(mx, 2)
    chip = mx // 2
    x_pos = lax.rem(chip, 2)
    y_pos = chip // 2
    others = (y_pos * 2 + (1 - x_pos), (1 - y_pos) * 2 + x_pos, (1 - y_pos) * 2 + (1 - x_pos))
    return core, chip, chip * 2 + (1 - core), others


def hbm(array):
    return pltpu.with_memory_space_constraint(array, pltpu.HBM)


def send(src, dst, send_sem, recv_sem, my, mx):
    copy = pltpu.make_async_remote_copy(src_ref=src, dst_ref=dst, send_sem=send_sem, recv_sem=recv_sem, device_id=(my, mx), device_id_type=MESH)
    copy.start()
    return copy


def drain(ref, sem):
    pltpu.make_async_copy(ref, ref, sem).wait()


def share_stat(square_sum, my, mx, stat_out, stat_in, send_sems, recv_sems):
    rows = square_sum.shape[0]
    turned = jnp.transpose(jnp.broadcast_to(square_sum, (rows, 128)))[0:8]
    stat_out[...] = turned
    copies = []
    for step in range(1, 8):
        peer = lax.rem(mx + step, 8)
        copies.append(send(stat_out, stat_in.at[mx], send_sems.at[step], recv_sems.at[step], my, peer))
    stat_in[mx] = turned
    for copy in copies:
        copy.wait()
    total = jnp.sum(stat_in[...], axis=0)
    return jnp.transpose(jnp.broadcast_to(total[0:1], (128, rows)))[:, 0:1]


def enter(my, mx, with_z):
    barrier = pltpu.get_barrier_semaphore()
    for step in range(1, 8):
        pl.semaphore_signal(barrier, inc=1, device_id=(my, lax.rem(mx + step, 8)), device_id_type=MESH)
    if with_z:
        pl.semaphore_signal(barrier, inc=1, device_id=(1 - my, mx), device_id_type=MESH)
    pl.semaphore_wait(barrier, 8 if with_z else 7)


def qkv_kernel(hidden, pieces, freq_ref, lens_hbm, x_hbm, gain_hbm, wq_hbm, wk_hbm, wv_hbm, out_ref, cos_ref, sin_ref,
               lens_s, x_v, gain_v, wq_v, wk_v, wv_v, part, pair_in, chip_in, stat_out, stat_in,
               w_sems, stat_send, stat_recv, pair_send, pair_recv, chip_send, chip_recv):
    my = lax.axis_index("my")
    mx = lax.axis_index("mx")
    core, chip, partner, others = neighbours(mx)
    loads = [pltpu.make_async_copy(src, dst, w_sems.at[n]) for n, (src, dst) in enumerate((
        (wq_hbm, wq_v), (wk_hbm, wk_v), (wv_hbm, wv_v), (x_hbm, x_v), (gain_hbm, gain_v), (lens_hbm, lens_s)))]
    for n in (3, 4, 5, 0, 1, 2):
        loads[n].start()
    enter(my, mx, False)
    loads[3].wait()
    x = x_v[...].astype(F32)
    square_sum = jnp.sum(x * x, axis=1, keepdims=True)
    loads[4].wait()
    loads[5].wait()
    rows = lens_s.shape[0]
    sub = lax.broadcasted_iota(jnp.int32, (rows, HEAD // 2), 0)
    position = jnp.zeros((rows, HEAD // 2), F32)
    for b in range(rows):
        position = jnp.where(sub == b, lens_s[b].astype(F32), position)
    angles = position * freq_ref[...][None, :]
    cos_half = jnp.cos(angles)
    sin_half = jnp.sin(angles)
    cos_ref[...] = jnp.concatenate([cos_half, cos_half], axis=1)
    sin_ref[...] = jnp.concatenate([-sin_half, sin_half], axis=1)
    stat = share_stat(square_sum, my, mx, stat_out, stat_in, stat_send, stat_recv)
    normed = (x * lax.rsqrt(stat / hidden + NORM_EPS) * gain_v[...].astype(F32)[None, :]).astype(BF16)
    weights = (wq_v, wk_v, wv_v)
    copies = []
    waited = set()
    pair_copies = []
    for n, (which, first, width, out_first) in enumerate(pieces):
        if which not in waited:
            loads[which].wait()
            waited.add(which)
        cols = pl.ds(out_first, width)
        product = jnp.dot(normed, weights[which][:, first:first + width], preferred_element_type=F32)
        part[:, :, :, cols] = product.reshape(4, 2, 8, width).astype(BF16)
        pair_copies.append(send(part.at[:, 1 - core, :, cols], pair_in.at[:, :, cols], pair_send.at[n], pair_recv.at[n], my, partner))
    for n, (which, first, width, out_first) in enumerate(pieces):
        cols = pl.ds(out_first, width)
        pair_copies[n].wait_recv()
        pair_in[:, :, cols] = (part[:, core, :, cols].astype(F32) + pair_in[:, :, cols].astype(F32)).astype(BF16)
        for k, other in enumerate(others):
            copies.append(send(pair_in.at[other, :, cols], chip_in.at[k, :, cols], chip_send.at[n, k], chip_recv.at[n, k], my, other * 2 + core))
    for n, (which, first, width, out_first) in enumerate(pieces):
        cols = pl.ds(out_first, width)
        total = pair_in[chip, :, cols].astype(F32)
        for k in range(3):
            copies[n * 3 + k].wait_recv()
            total = total + chip_in[k, :, cols].astype(F32)
        out_ref[:, cols] = total
    for copy in pair_copies + copies:
        copy.wait_send()


def attend_kernel(proj_ref, cos_ref, sin_ref, k_ref, v_ref, lens_hbm, bq_hbm, bk_hbm, bv_hbm, ko_hbm, vo_hbm, attn_ref,
                  lens_s, bq_v, bk_v, bv_v, q_s, k_s, v_s, o_s, k_win, v_win, small_sems, out_sems, win_sems):
    rows, slots, _ = k_ref.shape
    kv_heads = bk_v.shape[0] // HEAD
    heads = bq_v.shape[0] // HEAD
    group = heads // kv_heads
    q_cols = heads * HEAD
    kv_cols = kv_heads * HEAD
    smalls = [pltpu.make_async_copy(src, dst, small_sems.at[n]) for n, (src, dst) in enumerate(((bq_hbm, bq_v), (bk_hbm, bk_v), (bv_hbm, bv_v), (lens_hbm, lens_s)))]
    for small in smalls:
        small.start()
    outs = []
    for b in range(rows):
        outs.append((pltpu.make_async_copy(k_ref.at[b], ko_hbm.at[b], out_sems.at[0, b]), pltpu.make_async_copy(v_ref.at[b], vo_hbm.at[b], out_sems.at[1, b])))
        for out in outs[b]:
            out.start()
    cos = cos_ref[...]
    sin = sin_ref[...]
    q_s[...] = jnp.zeros_like(q_s)
    for small in smalls:
        small.wait()

    def biased(first, bias_ref, h):
        return proj_ref[:, first + h * HEAD:first + (h + 1) * HEAD] + bias_ref[h * HEAD:(h + 1) * HEAD].astype(F32)[None, :]

    def rotated(vals):
        return vals * cos + pltpu.roll(vals, HEAD // 2, 1) * sin

    for h in range(heads):
        q_s[:, h, :] = rotated(biased(0, bq_v, h))
    for h in range(kv_heads):
        k_new = rotated(biased(q_cols, bk_v, h))
        v_new = biased(q_cols + kv_cols, bv_v, h)
        for r in range(16 // kv_heads):
            k_s[:, r * kv_heads + h, :] = k_new
            v_s[:, r * kv_heads + h, :] = v_new
    q_pad = q_s.shape[1]
    per_tile = 16 // kv_heads
    sub = lax.broadcasted_iota(jnp.int32, (16, HEAD), 0) // kv_heads
    row = lax.broadcasted_iota(jnp.int32, (q_pad, 1), 0)
    row_head = sum((row >= group * n).astype(jnp.int32) for n in range(1, kv_heads))
    col = lax.broadcasted_iota(jnp.int32, (q_pad, slots), 1)
    offset = jnp.where(lax.rem(col, kv_heads) == row_head, col // kv_heads, slots)
    new_col = lax.broadcasted_iota(jnp.int32, (q_pad, 16), 1)

    def window(b, position):
        base = pl.multiple_of(position // per_tile * 16, 16)
        at_slot = sub == lax.rem(position, per_tile)
        for src, new, win in ((k_ref, k_s, k_win), (v_ref, v_s, v_win)):
            win[b] = jnp.where(at_slot, new[b], src[b, pl.ds(base, 16), :].astype(F32)).astype(BF16)

    def one_row(b):
        position = lens_s[b]
        window(b, position)
        query = q_s[b].astype(BF16)
        scores = lax.dot_general(query, k_ref[b], (((1,), (1,)), ((), ())), preferred_element_type=F32) * HEAD ** -0.5
        scores = jnp.where(offset < position, scores, -jnp.inf)
        new_scores = lax.dot_general(query, k_s[b].astype(BF16), (((1,), (1,)), ((), ())), preferred_element_type=F32) * HEAD ** -0.5
        new_scores = jnp.where(new_col == row_head, new_scores, -jnp.inf)
        top = jnp.maximum(jnp.max(scores, axis=1, keepdims=True), jnp.max(new_scores, axis=1, keepdims=True))
        weights = jnp.exp(scores - top)
        new_weights = jnp.exp(new_scores - top)
        weight_sum = jnp.sum(weights, axis=1, keepdims=True) + jnp.sum(new_weights, axis=1, keepdims=True)
        weighted = jnp.dot(weights.astype(BF16), v_ref[b], preferred_element_type=F32)
        weighted = weighted + jnp.dot(new_weights.astype(BF16), v_s[b].astype(BF16), preferred_element_type=F32)
        o_s[b] = weighted / weight_sum

    def fix(b):
        base = pl.multiple_of(lens_s[b] // per_tile * 16, 16)
        return [pltpu.make_async_copy(win.at[b], hbm_out.at[b, pl.ds(base, 16), :], win_sems.at[n, b]) for n, (win, hbm_out) in enumerate(((k_win, ko_hbm), (v_win, vo_hbm)))]

    @pl.loop(0, rows, unroll=8)
    def _(b):
        one_row(b)

    for b in range(rows):
        for out, win in zip(outs[b], fix(b)):
            out.wait()
            win.start()
    for h in range(heads):
        attn_ref[:, h * HEAD:(h + 1) * HEAD] = o_s[:, h, :].astype(BF16)
    for b in range(rows):
        for win in fix(b):
            win.wait()


def mlp_kernel(hidden, chunks, per_load, lags, attn_ref, x_hbm, gain_hbm, wo_hbm, wg_hbm, wu_hbm, wd_hbm, out_ref,
               x_v, gain_v, attn_all, wo_v, wg_v, wu_v, wd_v, z_out, z_in, stat_out, stat_in, h_v, m_v, acc, mine, theirs, pair_in, hop_in, fin_in, act,
               in_sems, wg_sems, wu_sems, wd_sems, ag_send, ag_recv, z_send, z_recv, stat_send, stat_recv,
               pair_send, pair_recv, hop_send, hop_recv, fin_send, fin_recv, near_send, near_recv, far_send, far_recv, fwd_send, fwd_recv):
    my = lax.axis_index("my")
    mx = lax.axis_index("mx")
    core, chip, partner, others = neighbours(mx)
    x_pos = lax.rem(chip, 2)
    y_pos = chip // 2
    x_peer = others[0] * 2 + core
    y_peer = others[1] * 2 + core
    half = 2 * act.shape[6]
    loads = chunks // per_load
    load_cols = per_load * 2 * half
    ring = wd_v.shape[0]

    firsts = [pltpu.make_async_copy(src, dst, in_sems.at[n]) for n, (src, dst) in enumerate(((wo_hbm, wo_v), (x_hbm, x_v), (gain_hbm, gain_v)))]
    for first in firsts:
        first.start()

    def load_gate(n):
        cols = pl.ds(pl.multiple_of(n * load_cols, 128), load_cols)
        return pltpu.make_async_copy(wg_hbm.at[:, cols], wg_v.at[n], wg_sems.at[n]), pltpu.make_async_copy(wu_hbm.at[:, cols], wu_v.at[n], wu_sems.at[n])

    def load_down(n):
        slot = lax.rem(n, ring)
        return pltpu.make_async_copy(wd_hbm.at[n], wd_v.at[slot], wd_sems.at[slot])

    @pl.loop(0, loads)
    def _(n):
        for load in load_gate(n):
            load.start()

    for n in range(ring):
        load_down(n).start()

    enter(my, mx, True)

    copies = []
    for step in range(1, 8):
        peer = lax.rem(mx + step, 8)
        copies.append(send(attn_ref, attn_all.at[mx], ag_send.at[step], ag_recv.at[step], my, peer))
    attn_all[mx] = attn_ref[...]
    for first in firsts:
        first.wait()
    for copy in copies:
        copy.wait()
    rows = x_v.shape[0]
    attn = attn_all[...].reshape(rows, attn_ref.shape[1])
    z_out[0] = jnp.dot(attn, wo_v[...], preferred_element_type=F32).astype(BF16)
    z_copy = send(z_out.at[0], z_in.at[0], z_send.at[0], z_recv.at[0], 1 - my, mx)
    z_copy.wait()
    mid = (x_v[...].astype(F32) + (z_out[0].astype(F32) + z_in[0].astype(F32))).astype(BF16)
    m_v[...] = mid
    mid = mid.astype(F32)
    stat = share_stat(jnp.sum(mid * mid, axis=1, keepdims=True), my, mx, stat_out, stat_in, stat_send, stat_recv)
    h_v[...] = (mid * lax.rsqrt(stat / hidden + NORM_EPS) * gain_v[...].astype(F32)[None, :]).astype(BF16)
    acc[...] = jnp.zeros_like(acc)

    def products(k, part, dest):
        n = k // per_load
        cols = pl.ds(pl.multiple_of(lax.rem(k, per_load) * (2 * half) + part * half, 128), half)
        h = h_v[...]
        for which, weights in ((0, wg_v), (1, wu_v)):
            out = jnp.dot(h, weights[n, :, cols], preferred_element_type=F32).astype(BF16)
            for way in range(2):
                dest[k, way, :, :, which] = out[:, way * half // 2:(way + 1) * half // 2].reshape(2, 2, 16, half // 2)

    def multiply(k):
        @pl.when(lax.rem(k, per_load) == 0)
        def _():
            for load in load_gate(k // per_load):
                load.wait()

        products(k, 1 - core, theirs)
        send(theirs.at[k], pair_in.at[k], pair_send.at[k], pair_recv.at[k], my, partner)
        products(k, core, mine)

    def scatter(k):
        drain(pair_in.at[k], pair_recv.at[k])
        pair_in[k] = (mine[k].astype(F32) + pair_in[k].astype(F32)).astype(BF16)
        send(pair_in.at[k, 0, :, 1 - x_pos], hop_in.at[k, 0], hop_send.at[k], hop_recv.at[k], my, x_peer)
        send(pair_in.at[k, 1, 1 - y_pos], hop_in.at[k, 1], hop_send.at[k], hop_recv.at[k], my, y_peer)

    def combine(k):
        drain(hop_in.at[k], hop_recv.at[k])
        hop_in[k, 0] = (pair_in[k, 0, :, x_pos].astype(F32) + hop_in[k, 0].astype(F32)).astype(BF16)
        hop_in[k, 1] = (pair_in[k, 1, y_pos].astype(F32) + hop_in[k, 1].astype(F32)).astype(BF16)
        send(hop_in.at[k, 0, 1 - y_pos], fin_in.at[k, 0], fin_send.at[k], fin_recv.at[k], my, y_peer)
        send(hop_in.at[k, 1, 1 - x_pos], fin_in.at[k, 1], fin_send.at[k], fin_recv.at[k], my, x_peer)

    def activate(k):
        drain(fin_in.at[k], fin_recv.at[k])
        for way, own in ((0, y_pos), (1, x_pos)):
            total = hop_in[k, way, own].astype(F32) + fin_in[k, way].astype(F32)
            gate = total[0]
            act[k, core, way, y_pos, x_pos] = (gate * jax.nn.sigmoid(gate) * total[1]).astype(BF16)
        for way, peer in ((0, y_peer), (1, x_peer)):
            block = act.at[k, core, way, y_pos, x_pos]
            send(block, block, near_send.at[k], near_recv.at[k], my, peer)
        both = act.at[k, core, :, y_pos, x_pos]
        send(both, both, fwd_send.at[k], fwd_recv.at[k], my, partner)

    def gather(k):
        drain(act.at[k, core, 0, 0], near_recv.at[k])
        for block, peer in ((act.at[k, core, 0, :, x_pos], x_peer), (act.at[k, core, 1, y_pos], y_peer)):
            send(block, block, far_send.at[k], far_recv.at[k], my, peer)
        for block in (act.at[k, core, 0, 1 - y_pos, x_pos], act.at[k, core, 1, y_pos, 1 - x_pos]):
            send(block, block, fwd_send.at[k], fwd_recv.at[k], my, partner)

    def forward(k):
        drain(act.at[k, core, 0], far_recv.at[k])
        for block in (act.at[k, core, 0, :, 1 - x_pos], act.at[k, core, 1, 1 - y_pos]):
            send(block, block, fwd_send.at[k], fwd_recv.at[k], my, partner)

    def contract(k):
        n = k // per_load
        step = lax.rem(k, per_load)

        @pl.when(step == 0)
        def _():
            load_down(n).wait()

        drain(act.at[k, 1 - core], fwd_recv.at[k])
        total = acc[...]
        for part in range(2):
            lhs = jnp.concatenate([act[k, part, way].reshape(rows, half // 2) for way in range(2)], axis=1)
            total = total + jnp.dot(lhs, wd_v[lax.rem(n, ring), step, part], preferred_element_type=F32)
        acc[...] = total

        @pl.when(jnp.logical_and(step == per_load - 1, n + ring < loads))
        def _():
            load_down(n + ring).start()

    stages = tuple(zip((contract, forward, gather, activate, combine, scatter, multiply), lags))

    @pl.loop(0, chunks + lags[0])
    def _(t):
        for stage, lag in stages:
            @pl.when(jnp.logical_and(t >= lag, t < chunks + lag))
            def _():
                stage(t - lag)

    z_out[1] = acc[...].astype(BF16)
    z_copy = send(z_out.at[1], z_in.at[1], z_send.at[1], z_recv.at[1], 1 - my, mx)
    z_copy.wait()
    out_ref[...] = (m_v[...].astype(F32) + (z_out[1].astype(F32) + z_in[1].astype(F32))).astype(BF16)

    @pl.loop(0, chunks)
    def _(k):
        drain(theirs.at[k], pair_send.at[k])
        drain(hop_in.at[k], hop_send.at[k])
        drain(fin_in.at[k], fin_send.at[k])
        drain(act.at[k, core, 0, 0], near_send.at[k])
        drain(act.at[k, core, 0], far_send.at[k])
        drain(act.at[k, core], fwd_send.at[k])


def solution(mesh):
    mx_size = mesh.shape["mx"]
    act_spec = P(None, "mx")
    cache_spec = P("mx", None, "my", None)
    in_specs = (act_spec, P("mx"), P("mx"), P("mx"), P("mx", "my"), P("my"), P("mx", "my"), P("my"), P("mx", "my"), P("my"), P("my", "mx"), P("mx", "my"), P("mx", "my"), P("my", "mx"), cache_spec, cache_spec)
    out_specs = (act_spec, cache_spec, cache_spec)
    vmem = pl.BlockSpec(memory_space=pltpu.VMEM)
    anywhere = pl.BlockSpec(memory_space=pl.ANY)

    def local_layer(x_in, seq_lens, gain_attn, gain_mlp, w_q, b_q, w_k, b_k, w_v, b_v, w_o, w_gate, w_up, w_down, k_cache, v_cache):
        rows, cols = x_in.shape
        hidden = cols * mx_size
        q_cols = w_q.shape[1]
        kv_cols = w_k.shape[1]
        heads = q_cols // HEAD
        kv_heads = kv_cols // HEAD
        local_rows = rows // mx_size
        qkv_cols = q_cols + 2 * kv_cols
        pieces = ((0, 0, q_cols // 2, 0), (0, q_cols // 2, q_cols // 2, q_cols // 2), (1, 0, kv_cols, q_cols), (2, 0, kv_cols, q_cols + kv_cols))
        inv_freq = ROPE_THETA ** (-2.0 * jnp.arange(HEAD // 2, dtype=F32) / HEAD)
        table = jax.ShapeDtypeStruct((local_rows, HEAD), F32)

        projected, cos_tab, sin_tab = pl.pallas_call(
            functools.partial(qkv_kernel, hidden, pieces),
            name="qkv",
            out_shape=(jax.ShapeDtypeStruct((local_rows, qkv_cols), F32), table, table),
            in_specs=[vmem] + [anywhere] * 6,
            out_specs=(vmem, vmem, vmem),
            scratch_shapes=[
                pltpu.SMEM((local_rows,), jnp.int32), VMEM((rows, cols), BF16), VMEM((cols,), BF16),
                VMEM(w_q.shape, BF16), VMEM(w_k.shape, BF16), VMEM(w_v.shape, BF16),
                VMEM((4, 2, local_rows, qkv_cols), BF16), VMEM((4, local_rows, qkv_cols), BF16), VMEM((3, local_rows, qkv_cols), BF16),
                VMEM((8, rows), F32), VMEM((8, 8, rows), F32),
                DMA((6,)), DMA((8,)), DMA((8,)), DMA((4,)), DMA((4,)), DMA((4, 3)), DMA((4, 3)),
            ],
            compiler_params=pltpu.CompilerParams(collective_id=0, has_side_effects=True, vmem_limit_bytes=16 * 2 ** 20),
            cost_estimate=pl.CostEstimate(flops=40_000_000_000, bytes_accessed=4_600_000, transcendentals=0),
        )(inv_freq, hbm(seq_lens), hbm(x_in), hbm(gain_attn), hbm(w_q), hbm(w_k), hbm(w_v))

        slots = k_cache.shape[1] * kv_heads
        flat = (local_rows, slots, HEAD)
        padded = (heads + 7) // 8 * 8
        k_flat, v_flat, attn = pl.pallas_call(
            attend_kernel,
            name="attend",
            out_shape=(jax.ShapeDtypeStruct(flat, BF16), jax.ShapeDtypeStruct(flat, BF16), jax.ShapeDtypeStruct((local_rows, q_cols), BF16)),
            in_specs=[vmem] * 5 + [anywhere] * 4,
            out_specs=(anywhere, anywhere, vmem),
            scratch_shapes=[
                pltpu.SMEM((local_rows,), jnp.int32), VMEM(b_q.shape, BF16), VMEM(b_k.shape, BF16), VMEM(b_v.shape, BF16),
                VMEM((local_rows, padded, HEAD), F32), VMEM((local_rows, 16, HEAD), F32), VMEM((local_rows, 16, HEAD), F32), VMEM((local_rows, padded, HEAD), F32),
                VMEM((local_rows, 16, HEAD), BF16), VMEM((local_rows, 16, HEAD), BF16),
                DMA((4,)), DMA((2, local_rows)), DMA((2, local_rows)),
            ],
            compiler_params=pltpu.CompilerParams(vmem_limit_bytes=26 * 2 ** 20),
            cost_estimate=pl.CostEstimate(flops=20_000_000_000, bytes_accessed=17_000_000, transcendentals=0),
        )(projected, cos_tab, sin_tab, pltpu.with_memory_space_constraint(k_cache.reshape(flat), VMEM), pltpu.with_memory_space_constraint(v_cache.reshape(flat), VMEM),
          hbm(seq_lens), hbm(b_q), hbm(b_k), hbm(b_v))

        ff_cols = w_gate.shape[1]
        half = 256
        chunks = ff_cols // (2 * half)
        per_load = 3
        ring = 3
        loads = chunks // per_load
        lags = (28, 25, 20, 14, 8, 2, 0)
        x_out = pl.pallas_call(
            functools.partial(mlp_kernel, hidden, chunks, per_load, lags),
            name="mlp",
            out_shape=jax.ShapeDtypeStruct((rows, cols), BF16),
            in_specs=[vmem] + [anywhere] * 6,
            out_specs=vmem,
            scratch_shapes=[
                VMEM((rows, cols), BF16), VMEM((cols,), BF16),
                VMEM((8, local_rows, q_cols), BF16), VMEM(w_o.shape, BF16),
                VMEM((loads, cols, per_load * 2 * half), BF16), VMEM((loads, cols, per_load * 2 * half), BF16), VMEM((ring, per_load, 2, half, cols), BF16),
                VMEM((2, rows, cols), BF16), VMEM((2, rows, cols), BF16), VMEM((8, rows), F32), VMEM((8, 8, rows), F32),
                VMEM((rows, cols), BF16), VMEM((rows, cols), BF16), VMEM((rows, cols), F32),
            ] + [VMEM((chunks, 2, 2, 2, 2, 16, half // 2), BF16)] * 3 + [
                VMEM((chunks, 2, 2, 2, 16, half // 2), BF16), VMEM((chunks, 2, 2, 16, half // 2), BF16), VMEM((chunks, 2, 2, 2, 2, 16, half // 2), BF16),
                DMA((3,)), DMA((loads,)), DMA((loads,)), DMA((ring,)), DMA((8,)), DMA((8,)), DMA((2,)), DMA((2,)), DMA((8,)), DMA((8,)),
            ] + [DMA((chunks,))] * 12,
            compiler_params=pltpu.CompilerParams(collective_id=1, has_side_effects=True, vmem_limit_bytes=int(52.5 * 2 ** 20)),
            cost_estimate=pl.CostEstimate(flops=60_000_000_000, bytes_accessed=57_000_000, transcendentals=0),
        )(attn, hbm(x_in), hbm(gain_mlp), hbm(w_o), hbm(w_gate), hbm(w_up), hbm(w_down.reshape(loads, per_load, 2, half, cols)))
        return x_out, k_flat.reshape(k_cache.shape), v_flat.reshape(v_cache.shape)

    return jax.shard_map(local_layer, mesh=mesh, in_specs=in_specs, out_specs=out_specs, check_vma=False)
```

time: 105 us -> 78.8 us (0.75)
  local copies, waits for them, and re-layouts: 14.5 us -> 0.65 us
  Pallas kernels: 88.5 us -> 77.3 us
    unnamed x23 -> x5, local copies, waits for them, and re-layouts: 13.2 us -> 0.65 us
    pallas_call x1, Pallas kernels: 63.8 us -> 54.9 us  [local_layer(): pl.pallas_call(functools.partial(mlp_kernel, hidden, chunks, per_load, la...]
    pallas_call x1, Pallas kernels: 9.33 us -> 7.66 us  [local_layer(): pl.pallas_call(attend_kernel, name='attend', out_shape=(jax.ShapeDtypeStr...]
    reshape x2 -> x0, local copies, waits for them, and re-layouts: 1.29 us -> none  [the longest x1 0.69 us: local_layer(): gain_attn.reshape(1, cols)]
where the time goes in v2:
time: 78.8 us; the launch traced here: 78.6 us
  Pallas kernels  77.3 us (98%)
    pallas_call x1, Pallas kernels, local_layer(): pl.pallas_call(functools.partial(mlp_kernel, hidden, chunks, per_load, la...  54.9 us
    pallas_call x1, Pallas kernels, local_layer(): pl.pallas_call(functools.partial(qkv_kernel, hidden, pieces), name='qkv',...  14.8 us
    pallas_call x1, Pallas kernels, local_layer(): pl.pallas_call(attend_kernel, name='attend', out_shape=(jax.ShapeDtypeStr...  7.66 us

profile of v2, /device:TPU:0, one launch (start us, length us, event | category | flops | bytes accessed | tf_op | source)
XLA Modules:
  0.0 78.6 jit_solution(605146809952319948)
XLA Ops:
  0.6 0.0 copy-start
  0.7 0.0 copy-start.1
  0.7 14.8 %qkv.1 = (f32[8,3584]{1,0:T(8,128)S(1)}, f32[8,128]{1,0:T(8,128)S(1)}, f32[8,128]{1,0:T(8,128)S(1)}) custom-call(f32[64]{0:T(128)S(1)} %multiply_power_fusion.freq_ref, s32[8]{0:T(128)} %lens_hbm.3, bf16[64,640]{1,0:T(8,128)(2,1)} %x_hbm.3, bf16[640]{0:T(1024)(128)(2,1)} %gain_hbm.2, bf16[640,2560]{1,0:T(8,128)(2,1)} %wq_hbm.1, bf16[640,512]{1,0:T(8,128)(2,1)} %wk_hbm.1, ...), custom_call_target="tpu_custom_call" | custom-call | flops 40000000000 | bytes 4600000 | tf_op jit(solution)/shard_map/qkv/pallas_call | solution.py:390
  15.5 0.0 copy-done
  15.5 0.0 copy-done.1
  15.5 7.7 %attend.1 = (bf16[8,4096,128]{2,1,0:T(8,128)(2,1)}, bf16[8,4096,128]{2,1,0:T(8,128)(2,1)}, bf16[8,2560]{1,0:T(8,128)(2,1)S(1)}) custom-call(f32[8,3584]{1,0:T(8,128)S(1)} %get-tuple-element.9.proj_ref, f32[8,128]{1,0:T(8,128)S(1)} %get-tuple-element.10.cos_ref, f32[8,128]{1,0:T(8,128)S(1)} %get-tuple-element.11.sin_ref, bf16[8,4096,128]{2,1,0:T(8,128)(2,1)S(1)} %bitcast.5, ...), custom_call_target="tpu_custom_call" | custom-call | flops 20000000000 | bytes 17000000 | tf_op jit(solution)/shard_map/attend/pallas_call | solution.py:410
  23.1 54.9 %mlp.1 = bf16[64,640]{1,0:T(8,128)(2,1)S(1)} custom-call(bf16[8,2560]{1,0:T(8,128)(2,1)S(1)} %get-tuple-element.12.attn_ref, bf16[64,640]{1,0:T(8,128)(2,1)} %x_hbm.3, bf16[640]{0:T(1024)(128)(2,1)} %gain_hbm.3, bf16[2560,640]{1,0:T(8,128)(2,1)} %wo_hbm.1, bf16[640,13824]{1,0:T(8,128)(2,1)} %wg_hbm.1, bf16[640,13824]{1,0:T(8,128)(2,1)} %wu_hbm.1, ...), custom_call_target="tpu_custom_call" | custom-call | flops 60000002048 | bytes 57000000 | tf_op jit(solution)/shard_map/mlp/pallas_call | solution.py:434
  78.0 0.6 copy.20
  (1 shorter events, 0.0 us)
Async XLA Ops:
  0.6 14.8 %copy-start = (bf16[8,1024,4,128]{3,2,1,0:T(4,128)(2,1)S(1)}, bf16[8,1024,4,128]{3,2,1,0:T(4,128)(2,1)}, u32[]{:S(2)}) copy-start(bf16[8,1024,4,128]{3,2,1,0:T(4,128)(2,1)} %param.30) | copy-start | bytes 25165828
  0.7 14.8 %copy-start.1 = (bf16[8,1024,4,128]{3,2,1,0:T(4,128)(2,1)S(1)}, bf16[8,1024,4,128]{3,2,1,0:T(4,128)(2,1)}, u32[]{:S(2)}) copy-start(bf16[8,1024,4,128]{3,2,1,0:T(4,128)(2,1)} %param.31) | copy-start | bytes 25165828

commit v3 on v2

--- a/solution.py
+++ b/solution.py
@@ -40,7 +40,7 @@
     pltpu.make_async_copy(ref, ref, sem).wait()
 
 
-def share_stat(square_sum, my, mx, stat_out, stat_in, send_sems, recv_sems):
+def share_stat(square_sum, my, mx, stat_out, stat_in, send_sems, recv_sems, between=None):
     rows = square_sum.shape[0]
     turned = jnp.transpose(jnp.broadcast_to(square_sum, (rows, 128)))[0:8]
     stat_out[...] = turned
@@ -49,57 +49,62 @@
         peer = lax.rem(mx + step, 8)
         copies.append(send(stat_out, stat_in.at[mx], send_sems.at[step], recv_sems.at[step], my, peer))
     stat_in[mx] = turned
+    if between is not None:
+        between()
     for copy in copies:
         copy.wait()
     total = jnp.sum(stat_in[...], axis=0)
     return jnp.transpose(jnp.broadcast_to(total[0:1], (128, rows)))[:, 0:1]
 
 
-def enter(my, mx, with_z):
+def enter(my, mx, with_z, meanwhile=None):
     barrier = pltpu.get_barrier_semaphore()
     for step in range(1, 8):
         pl.semaphore_signal(barrier, inc=1, device_id=(my, lax.rem(mx + step, 8)), device_id_type=MESH)
     if with_z:
         pl.semaphore_signal(barrier, inc=1, device_id=(1 - my, mx), device_id_type=MESH)
+    if meanwhile is not None:
+        meanwhile()
     pl.semaphore_wait(barrier, 8 if with_z else 7)
 
 
-def qkv_kernel(hidden, pieces, freq_ref, lens_hbm, x_hbm, gain_hbm, wq_hbm, wk_hbm, wv_hbm, out_ref, cos_ref, sin_ref,
-               lens_s, x_v, gain_v, wq_v, wk_v, wv_v, part, pair_in, chip_in, stat_out, stat_in,
+def qkv_kernel(hidden, pieces, freq_ref, lens_hbm, x_hbm, gain_hbm, wq_hbm, wk_hbm, wv_hbm, bq_hbm, bk_hbm, bv_hbm, out_ref,
+               lens_s, x_v, gain_v, wq_v, wk_v, wv_v, bq_v, bk_v, bv_v, cos_v, sin_v, part, pair_in, chip_in, stat_out, stat_in,
                w_sems, stat_send, stat_recv, pair_send, pair_recv, chip_send, chip_recv):
     my = lax.axis_index("my")
     mx = lax.axis_index("mx")
     core, chip, partner, others = neighbours(mx)
     loads = [pltpu.make_async_copy(src, dst, w_sems.at[n]) for n, (src, dst) in enumerate((
-        (wq_hbm, wq_v), (wk_hbm, wk_v), (wv_hbm, wv_v), (x_hbm, x_v), (gain_hbm, gain_v), (lens_hbm, lens_s)))]
-    for n in (3, 4, 5, 0, 1, 2):
+        (wq_hbm, wq_v), (wk_hbm, wk_v), (wv_hbm, wv_v), (x_hbm, x_v), (gain_hbm, gain_v), (lens_hbm, lens_s), (bq_hbm, bq_v), (bk_hbm, bk_v), (bv_hbm, bv_v)))]
+    for n in (3, 4, 5, 0, 1, 2, 6, 7, 8):
         loads[n].start()
-    enter(my, mx, False)
-    loads[3].wait()
+    enter(my, mx, False, loads[3].wait)
     x = x_v[...].astype(F32)
     square_sum = jnp.sum(x * x, axis=1, keepdims=True)
-    loads[4].wait()
-    loads[5].wait()
-    rows = lens_s.shape[0]
-    sub = lax.broadcasted_iota(jnp.int32, (rows, HEAD // 2), 0)
-    position = jnp.zeros((rows, HEAD // 2), F32)
-    for b in range(rows):
-        position = jnp.where(sub == b, lens_s[b].astype(F32), position)
-    angles = position * freq_ref[...][None, :]
-    cos_half = jnp.cos(angles)
-    sin_half = jnp.sin(angles)
-    cos_ref[...] = jnp.concatenate([cos_half, cos_half], axis=1)
-    sin_ref[...] = jnp.concatenate([-sin_half, sin_half], axis=1)
-    stat = share_stat(square_sum, my, mx, stat_out, stat_in, stat_send, stat_recv)
+
+    def tables():
+        loads[4].wait()
+        loads[5].wait()
+        rows = lens_s.shape[0]
+        sub = lax.broadcasted_iota(jnp.int32, (rows, HEAD // 2), 0)
+        position = jnp.zeros((rows, HEAD // 2), F32)
+        for b in range(rows):
+            position = jnp.where(sub == b, lens_s[b].astype(F32), position)
+        angles = position * freq_ref[...][None, :]
+        cos_half = jnp.cos(angles)
+        sin_half = jnp.sin(angles)
+        cos_v[...] = jnp.concatenate([cos_half, cos_half], axis=1)
+        sin_v[...] = jnp.concatenate([-sin_half, sin_half], axis=1)
+        for n in (0, 1, 2, 6, 7, 8):
+            loads[n].wait()
+
+    stat = share_stat(square_sum, my, mx, stat_out, stat_in, stat_send, stat_recv, tables)
     normed = (x * lax.rsqrt(stat / hidden + NORM_EPS) * gain_v[...].astype(F32)[None, :]).astype(BF16)
     weights = (wq_v, wk_v, wv_v)
+    biases = (bq_v, bk_v, bv_v)
     copies = []
-    waited = set()
     pair_copies = []
     for n, (which, first, width, out_first) in enumerate(pieces):
-        if which not in waited:
-            loads[which].wait()
-            waited.add(which)
         cols = pl.ds(out_first, width)
         product = jnp.dot(normed, weights[which][:, first:first + width], preferred_element_type=F32)
         part[:, :, :, cols] = product.reshape(4, 2, 8, width).astype(BF16)
@@ -116,47 +121,40 @@
         for k in range(3):
             copies[n * 3 + k].wait_recv()
             total = total + chip_in[k, :, cols].astype(F32)
-        out_ref[:, cols] = total
+        total = total + biases[which][first:first + width].astype(F32)[None, :]
+        for h in range(0, width, HEAD):
+            vals = total[:, h:h + HEAD]
+            if which < 2:
+                vals = vals * cos_v[...] + pltpu.roll(vals, HEAD // 2, 1) * sin_v[...]
+            out_ref[:, out_first + h:out_first + h + HEAD] = vals
     for copy in pair_copies + copies:
         copy.wait_send()
 
 
-def attend_kernel(proj_ref, cos_ref, sin_ref, k_ref, v_ref, lens_hbm, bq_hbm, bk_hbm, bv_hbm, ko_hbm, vo_hbm, attn_ref,
-                  lens_s, bq_v, bk_v, bv_v, q_s, k_s, v_s, o_s, k_win, v_win, small_sems, out_sems, win_sems):
+def attend_kernel(heads, proj_ref, k_ref, v_ref, lens_hbm, ko_hbm, vo_hbm, attn_ref,
+                  lens_s, q_s, k_s, v_s, o_s, k_win, v_win, lens_sem, out_sems, win_sems):
     rows, slots, _ = k_ref.shape
-    kv_heads = bk_v.shape[0] // HEAD
-    heads = bq_v.shape[0] // HEAD
+    q_cols = heads * HEAD
+    kv_cols = (proj_ref.shape[1] - q_cols) // 2
+    kv_heads = kv_cols // HEAD
     group = heads // kv_heads
-    q_cols = heads * HEAD
-    kv_cols = kv_heads * HEAD
-    smalls = [pltpu.make_async_copy(src, dst, small_sems.at[n]) for n, (src, dst) in enumerate(((bq_hbm, bq_v), (bk_hbm, bk_v), (bv_hbm, bv_v), (lens_hbm, lens_s)))]
-    for small in smalls:
-        small.start()
+    load_lens = pltpu.make_async_copy(lens_hbm, lens_s, lens_sem)
+    load_lens.start()
     outs = []
     for b in range(rows):
         outs.append((pltpu.make_async_copy(k_ref.at[b], ko_hbm.at[b], out_sems.at[0, b]), pltpu.make_async_copy(v_ref.at[b], vo_hbm.at[b], out_sems.at[1, b])))
         for out in outs[b]:
             out.start()
-    cos = cos_ref[...]
-    sin = sin_ref[...]
     q_s[...] = jnp.zeros_like(q_s)
-    for small in smalls:
-        small.wait()
-
-    def biased(first, bias_ref, h):
-        return proj_ref[:, first + h * HEAD:first + (h + 1) * HEAD] + bias_ref[h * HEAD:(h + 1) * HEAD].astype(F32)[None, :]
-
-    def rotated(vals):
-        return vals * cos + pltpu.roll(vals, HEAD // 2, 1) * sin
-
     for h in range(heads):
-        q_s[:, h, :] = rotated(biased(0, bq_v, h))
+        q_s[:, h, :] = proj_ref[:, h * HEAD:(h + 1) * HEAD]
     for h in range(kv_heads):
-        k_new = rotated(biased(q_cols, bk_v, h))
-        v_new = biased(q_cols + kv_cols, bv_v, h)
+        k_new = proj_ref[:, q_cols + h * HEAD:q_cols + (h + 1) * HEAD]
+        v_new = proj_ref[:, q_cols + kv_cols + h * HEAD:q_cols + kv_cols + (h + 1) * HEAD]
         for r in range(16 // kv_heads):
             k_s[:, r * kv_heads + h, :] = k_new
             v_s[:, r * kv_heads + h, :] = v_new
+    load_lens.wait()
     q_pad = q_s.shape[1]
     per_tile = 16 // kv_heads
     sub = lax.broadcasted_iota(jnp.int32, (16, HEAD), 0) // kv_heads
@@ -174,7 +172,8 @@
 
     def one_row(b):
         position = lens_s[b]
-        window(b, position)
+        if b < rows - 1:
+            window(b, position)
         query = q_s[b].astype(BF16)
         scores = lax.dot_general(query, k_ref[b], (((1,), (1,)), ((), ())), preferred_element_type=F32) * HEAD ** -0.5
         scores = jnp.where(offset < position, scores, -jnp.inf)
@@ -192,14 +191,14 @@
         base = pl.multiple_of(lens_s[b] // per_tile * 16, 16)
         return [pltpu.make_async_copy(win.at[b], hbm_out.at[b, pl.ds(base, 16), :], win_sems.at[n, b]) for n, (win, hbm_out) in enumerate(((k_win, ko_hbm), (v_win, vo_hbm)))]
 
-    @pl.loop(0, rows, unroll=8)
-    def _(b):
+    for b in range(rows - 1):
         one_row(b)
-
+    window(rows - 1, lens_s[rows - 1])
     for b in range(rows):
         for out, win in zip(outs[b], fix(b)):
             out.wait()
             win.start()
+    one_row(rows - 1)
     for h in range(heads):
         attn_ref[:, h * HEAD:(h + 1) * HEAD] = o_s[:, h, :].astype(BF16)
     for b in range(rows):
@@ -221,7 +220,7 @@
     half = 2 * act.shape[6]
     loads = chunks // per_load
     load_cols = per_load * 2 * half
-    ring = wd_v.shape[0]
+    ring = wg_v.shape[0]
 
     firsts = [pltpu.make_async_copy(src, dst, in_sems.at[n]) for n, (src, dst) in enumerate(((wo_hbm, wo_v), (x_hbm, x_v), (gain_hbm, gain_v)))]
     for first in firsts:
@@ -229,18 +228,19 @@
 
     def load_gate(n):
         cols = pl.ds(pl.multiple_of(n * load_cols, 128), load_cols)
-        return pltpu.make_async_copy(wg_hbm.at[:, cols], wg_v.at[n], wg_sems.at[n]), pltpu.make_async_copy(wu_hbm.at[:, cols], wu_v.at[n], wu_sems.at[n])
+        slot = lax.rem(n, ring)
+        return pltpu.make_async_copy(wg_hbm.at[:, cols], wg_v.at[slot], wg_sems.at[slot]), pltpu.make_async_copy(wu_hbm.at[:, cols], wu_v.at[slot], wu_sems.at[slot])
 
     def load_down(n):
-        slot = lax.rem(n, ring)
-        return pltpu.make_async_copy(wd_hbm.at[n], wd_v.at[slot], wd_sems.at[slot])
-
-    @pl.loop(0, loads)
+        return pltpu.make_async_copy(wd_hbm.at[n], wd_v.at[n], wd_sems.at[n])
+
+    @pl.loop(0, ring)
     def _(n):
         for load in load_gate(n):
             load.start()
 
-    for n in range(ring):
+    @pl.loop(0, loads)
+    def _(n):
         load_down(n).start()
 
     enter(my, mx, True)
@@ -266,24 +266,33 @@
     h_v[...] = (mid * lax.rsqrt(stat / hidden + NORM_EPS) * gain_v[...].astype(F32)[None, :]).astype(BF16)
     acc[...] = jnp.zeros_like(acc)
 
-    def products(k, part, dest):
+    def multiply(k):
         n = k // per_load
-        cols = pl.ds(pl.multiple_of(lax.rem(k, per_load) * (2 * half) + part * half, 128), half)
+        slot = lax.rem(n, ring)
+        step = lax.rem(k, per_load)
+
+        @pl.when(step == 0)
+        def _():
+            for load in load_gate(n):
+                load.wait()
+
         h = h_v[...]
-        for which, weights in ((0, wg_v), (1, wu_v)):
-            out = jnp.dot(h, weights[n, :, cols], preferred_element_type=F32).astype(BF16)
-            for way in range(2):
-                dest[k, way, :, :, which] = out[:, way * half // 2:(way + 1) * half // 2].reshape(2, 2, 16, half // 2)
-
-    def multiply(k):
-        @pl.when(lax.rem(k, per_load) == 0)
+
+        def products(part, dest):
+            cols = pl.ds(pl.multiple_of(step * (2 * half) + part * half, 128), half)
+            for which, weights in ((0, wg_v), (1, wu_v)):
+                out = jnp.dot(h, weights[slot, :, cols], preferred_element_type=F32).astype(BF16)
+                for way in range(2):
+                    dest[k, way, :, :, which] = out[:, way * half // 2:(way + 1) * half // 2].reshape(2, 2, 16, half // 2)
+
+        products(1 - core, theirs)
+        send(theirs.at[k], pair_in.at[k], pair_send.at[k], pair_recv.at[k], my, partner)
+        products(core, mine)
+
+        @pl.when(jnp.logical_and(step == per_load - 1, n + ring < loads))
         def _():
-            for load in load_gate(k // per_load):
-                load.wait()
-
-        products(k, 1 - core, theirs)
-        send(theirs.at[k], pair_in.at[k], pair_send.at[k], pair_recv.at[k], my, partner)
-        products(k, core, mine)
+            for load in load_gate(n + ring):
+                load.start()
 
     def scatter(k):
         drain(pair_in.at[k], pair_recv.at[k])
@@ -334,12 +343,8 @@
         total = acc[...]
         for part in range(2):
             lhs = jnp.concatenate([act[k, part, way].reshape(rows, half // 2) for way in range(2)], axis=1)
-            total = total + jnp.dot(lhs, wd_v[lax.rem(n, ring), step, part], preferred_element_type=F32)
+            total = total + jnp.dot(lhs, wd_v[n, step, part], preferred_element_type=F32)
         acc[...] = total
-
-        @pl.when(jnp.logical_and(step == per_load - 1, n + ring < loads))
-        def _():
-            load_down(n + ring).start()
 
     stages = tuple(zip((contract, forward, gather, activate, combine, scatter, multiply), lags))
 
@@ -385,52 +390,51 @@
         qkv_cols = q_cols + 2 * kv_cols
         pieces = ((0, 0, q_cols // 2, 0), (0, q_cols // 2, q_cols // 2, q_cols // 2), (1, 0, kv_cols, q_cols), (2, 0, kv_cols, q_cols + kv_cols))
         inv_freq = ROPE_THETA ** (-2.0 * jnp.arange(HEAD // 2, dtype=F32) / HEAD)
-        table = jax.ShapeDtypeStruct((local_rows, HEAD), F32)
-
-        projected, cos_tab, sin_tab = pl.pallas_call(
+
+        projected = pl.pallas_call(
             functools.partial(qkv_kernel, hidden, pieces),
             name="qkv",
-            out_shape=(jax.ShapeDtypeStruct((local_rows, qkv_cols), F32), table, table),
-            in_specs=[vmem] + [anywhere] * 6,
-            out_specs=(vmem, vmem, vmem),
+            out_shape=jax.ShapeDtypeStruct((local_rows, qkv_cols), F32),
+            in_specs=[vmem] + [anywhere] * 9,
+            out_specs=vmem,
             scratch_shapes=[
                 pltpu.SMEM((local_rows,), jnp.int32), VMEM((rows, cols), BF16), VMEM((cols,), BF16),
-                VMEM(w_q.shape, BF16), VMEM(w_k.shape, BF16), VMEM(w_v.shape, BF16),
+                VMEM(w_q.shape, BF16), VMEM(w_k.shape, BF16), VMEM(w_v.shape, BF16), VMEM(b_q.shape, BF16), VMEM(b_k.shape, BF16), VMEM(b_v.shape, BF16),
+                VMEM((local_rows, HEAD), F32), VMEM((local_rows, HEAD), F32),
                 VMEM((4, 2, local_rows, qkv_cols), BF16), VMEM((4, local_rows, qkv_cols), BF16), VMEM((3, local_rows, qkv_cols), BF16),
                 VMEM((8, rows), F32), VMEM((8, 8, rows), F32),
-                DMA((6,)), DMA((8,)), DMA((8,)), DMA((4,)), DMA((4,)), DMA((4, 3)), DMA((4, 3)),
+                DMA((9,)), DMA((8,)), DMA((8,)), DMA((4,)), DMA((4,)), DMA((4, 3)), DMA((4, 3)),
             ],
             compiler_params=pltpu.CompilerParams(collective_id=0, has_side_effects=True, vmem_limit_bytes=16 * 2 ** 20),
             cost_estimate=pl.CostEstimate(flops=40_000_000_000, bytes_accessed=4_600_000, transcendentals=0),
-        )(inv_freq, hbm(seq_lens), hbm(x_in), hbm(gain_attn), hbm(w_q), hbm(w_k), hbm(w_v))
+        )(inv_freq, hbm(seq_lens), hbm(x_in), hbm(gain_attn), hbm(w_q), hbm(w_k), hbm(w_v), hbm(b_q), hbm(b_k), hbm(b_v))
 
         slots = k_cache.shape[1] * kv_heads
         flat = (local_rows, slots, HEAD)
         padded = (heads + 7) // 8 * 8
         k_flat, v_flat, attn = pl.pallas_call(
-            attend_kernel,
+            functools.partial(attend_kernel, heads),
             name="attend",
             out_shape=(jax.ShapeDtypeStruct(flat, BF16), jax.ShapeDtypeStruct(flat, BF16), jax.ShapeDtypeStruct((local_rows, q_cols), BF16)),
-            in_specs=[vmem] * 5 + [anywhere] * 4,
+            in_specs=[vmem] * 3 + [anywhere],
             out_specs=(anywhere, anywhere, vmem),
             scratch_shapes=[
-                pltpu.SMEM((local_rows,), jnp.int32), VMEM(b_q.shape, BF16), VMEM(b_k.shape, BF16), VMEM(b_v.shape, BF16),
+                pltpu.SMEM((local_rows,), jnp.int32),
                 VMEM((local_rows, padded, HEAD), F32), VMEM((local_rows, 16, HEAD), F32), VMEM((local_rows, 16, HEAD), F32), VMEM((local_rows, padded, HEAD), F32),
                 VMEM((local_rows, 16, HEAD), BF16), VMEM((local_rows, 16, HEAD), BF16),
-                DMA((4,)), DMA((2, local_rows)), DMA((2, local_rows)),
+                DMA, DMA((2, local_rows)), DMA((2, local_rows)),
             ],
             compiler_params=pltpu.CompilerParams(vmem_limit_bytes=26 * 2 ** 20),
             cost_estimate=pl.CostEstimate(flops=20_000_000_000, bytes_accessed=17_000_000, transcendentals=0),
-        )(projected, cos_tab, sin_tab, pltpu.with_memory_space_constraint(k_cache.reshape(flat), VMEM), pltpu.with_memory_space_constraint(v_cache.reshape(flat), VMEM),
-          hbm(seq_lens), hbm(b_q), hbm(b_k), hbm(b_v))
+        )(projected, pltpu.with_memory_space_constraint(k_cache.reshape(flat), VMEM), pltpu.with_memory_space_constraint(v_cache.reshape(flat), VMEM), hbm(seq_lens))
 
         ff_cols = w_gate.shape[1]
-        half = 256
+        half = 768
         chunks = ff_cols // (2 * half)
-        per_load = 3
-        ring = 3
+        per_load = 1
+        ring = 6
         loads = chunks // per_load
-        lags = (28, 25, 20, 14, 8, 2, 0)
+        lags = (20, 17, 13, 9, 5, 2, 0)
         x_out = pl.pallas_call(
             functools.partial(mlp_kernel, hidden, chunks, per_load, lags),
             name="mlp",
@@ -440,12 +444,12 @@
             scratch_shapes=[
                 VMEM((rows, cols), BF16), VMEM((cols,), BF16),
                 VMEM((8, local_rows, q_cols), BF16), VMEM(w_o.shape, BF16),
-                VMEM((loads, cols, per_load * 2 * half), BF16), VMEM((loads, cols, per_load * 2 * half), BF16), VMEM((ring, per_load, 2, half, cols), BF16),
+                VMEM((ring, cols, per_load * 2 * half), BF16), VMEM((ring, cols, per_load * 2 * half), BF16), VMEM((loads, per_load, 2, half, cols), BF16),
                 VMEM((2, rows, cols), BF16), VMEM((2, rows, cols), BF16), VMEM((8, rows), F32), VMEM((8, 8, rows), F32),
                 VMEM((rows, cols), BF16), VMEM((rows, cols), BF16), VMEM((rows, cols), F32),
             ] + [VMEM((chunks, 2, 2, 2, 2, 16, half // 2), BF16)] * 3 + [
                 VMEM((chunks, 2, 2, 2, 16, half // 2), BF16), VMEM((chunks, 2, 2, 16, half // 2), BF16), VMEM((chunks, 2, 2, 2, 2, 16, half // 2), BF16),
-                DMA((3,)), DMA((loads,)), DMA((loads,)), DMA((ring,)), DMA((8,)), DMA((8,)), DMA((2,)), DMA((2,)), DMA((8,)), DMA((8,)),
+                DMA((3,)), DMA((ring,)), DMA((ring,)), DMA((loads,)), DMA((8,)), DMA((8,)), DMA((2,)), DMA((2,)), DMA((8,)), DMA((8,)),
             ] + [DMA((chunks,))] * 12,
             compiler_params=pltpu.CompilerParams(collective_id=1, has_side_effects=True, vmem_limit_bytes=int(52.5 * 2 ** 20)),
             cost_estimate=pl.CostEstimate(flops=60_000_000_000, bytes_accessed=57_000_000, transcendentals=0),

time: 78.8 us -> 71.5 us (0.907)
  Pallas kernels: 77.3 us -> 70.1 us
    pallas_call x1, Pallas kernels: 54.9 us -> 48.4 us  [local_layer(): pl.pallas_call(functools.partial(mlp_kernel, hidden, chunks, per_load, la...]
where the time goes in v3:
time: 71.5 us; the launch traced here: 71.4 us
  Pallas kernels  70.1 us (98%)
    pallas_call x1, Pallas kernels, local_layer(): pl.pallas_call(functools.partial(mlp_kernel, hidden, chunks, per_load, la...  48.4 us
    pallas_call x1, Pallas kernels, local_layer(): pl.pallas_call(functools.partial(qkv_kernel, hidden, pieces), name='qkv',...  14.7 us
    pallas_call x1, Pallas kernels, local_layer(): pl.pallas_call(functools.partial(attend_kernel, heads), name='attend', ou...  7.02 us

profile of v3, /device:TPU:0, one launch (start us, length us, event | category | flops | bytes accessed | tf_op | source)
XLA Modules:
  0.0 71.4 jit_solution(7880138301104470172)
XLA Ops:
  0.6 0.0 copy-start
  0.7 0.0 copy-start.1
  0.7 14.7 %qkv.1.proj_ref = f32[8,3584]{1,0:T(8,128)S(1)} custom-call(f32[64]{0:T(128)S(1)} %multiply_power_fusion.freq_ref, s32[8]{0:T(128)} %lens_hbm.3, bf16[64,640]{1,0:T(8,128)(2,1)} %x_hbm.3, bf16[640]{0:T(1024)(128)(2,1)} %gain_hbm.2, bf16[640,2560]{1,0:T(8,128)(2,1)} %wq_hbm.1, bf16[640,512]{1,0:T(8,128)(2,1)} %wk_hbm.1, bf16[640,512]{1,0:T(8,128)(2,1)} %wv_hbm.1, ...), custom_call_target="tpu_custom_call" | custom-call | flops 40000000000 | bytes 4600000 | tf_op jit(solution)/shard_map/qkv/pallas_call | solution.py:394
  15.4 0.0 copy-done
  15.4 0.0 copy-done.1
  15.4 7.0 %attend.1 = (bf16[8,4096,128]{2,1,0:T(8,128)(2,1)}, bf16[8,4096,128]{2,1,0:T(8,128)(2,1)}, bf16[8,2560]{1,0:T(8,128)(2,1)S(1)}) custom-call(f32[8,3584]{1,0:T(8,128)S(1)} %qkv.1.proj_ref, bf16[8,4096,128]{2,1,0:T(8,128)(2,1)S(1)} %bitcast.5, bf16[8,4096,128]{2,1,0:T(8,128)(2,1)S(1)} %bitcast.6, s32[8]{0:T(128)} %lens_hbm.3), custom_call_target="tpu_custom_call" | custom-call | flops 20000000000 | bytes 17000000 | tf_op jit(solution)/shard_map/attend/pallas_call | solution.py:415
  22.4 48.4 %mlp.1 = bf16[64,640]{1,0:T(8,128)(2,1)S(1)} custom-call(bf16[8,2560]{1,0:T(8,128)(2,1)S(1)} %get-tuple-element.6.attn_ref, bf16[64,640]{1,0:T(8,128)(2,1)} %x_hbm.3, bf16[640]{0:T(1024)(128)(2,1)} %gain_hbm.3, bf16[2560,640]{1,0:T(8,128)(2,1)} %wo_hbm.1, bf16[640,13824]{1,0:T(8,128)(2,1)} %wg_hbm.1, bf16[640,13824]{1,0:T(8,128)(2,1)} %wu_hbm.1, ...), custom_call_target="tpu_custom_call" | custom-call | flops 60000002048 | bytes 57000000 | tf_op jit(solution)/shard_map/mlp/pallas_call | solution.py:438
  70.8 0.6 copy.20
  (1 shorter events, 0.0 us)
Async XLA Ops:
  0.6 14.7 %copy-start = (bf16[8,1024,4,128]{3,2,1,0:T(4,128)(2,1)S(1)}, bf16[8,1024,4,128]{3,2,1,0:T(4,128)(2,1)}, u32[]{:S(2)}) copy-start(bf16[8,1024,4,128]{3,2,1,0:T(4,128)(2,1)} %param.30) | copy-start | bytes 25165828
  0.7 14.7 %copy-start.1 = (bf16[8,1024,4,128]{3,2,1,0:T(4,128)(2,1)S(1)}, bf16[8,1024,4,128]{3,2,1,0:T(4,128)(2,1)}, u32[]{:S(2)}) copy-start(bf16[8,1024,4,128]{3,2,1,0:T(4,128)(2,1)} %param.31) | copy-start | bytes 25165828

commit v4 on v3

--- a/solution.py
+++ b/solution.py
@@ -26,6 +26,11 @@
     return core, chip, chip * 2 + (1 - core), others
 
 
+def far_first(mx):
+    core, chip, partner, others = neighbours(mx)
+    return [other * 2 + c for other in (others[2], others[0], others[1]) for c in (core, 1 - core)] + [partner]
+
+
 def hbm(array):
     return pltpu.with_memory_space_constraint(array, pltpu.HBM)
 
@@ -45,8 +50,7 @@
     turned = jnp.transpose(jnp.broadcast_to(square_sum, (rows, 128)))[0:8]
     stat_out[...] = turned
     copies = []
-    for step in range(1, 8):
-        peer = lax.rem(mx + step, 8)
+    for step, peer in enumerate(far_first(mx)):
         copies.append(send(stat_out, stat_in.at[mx], send_sems.at[step], recv_sems.at[step], my, peer))
     stat_in[mx] = turned
     if between is not None:
@@ -69,16 +73,21 @@
 
 
 def qkv_kernel(hidden, pieces, freq_ref, lens_hbm, x_hbm, gain_hbm, wq_hbm, wk_hbm, wv_hbm, bq_hbm, bk_hbm, bv_hbm, out_ref,
-               lens_s, x_v, gain_v, wq_v, wk_v, wv_v, bq_v, bk_v, bv_v, cos_v, sin_v, part, pair_in, chip_in, stat_out, stat_in,
-               w_sems, stat_send, stat_recv, pair_send, pair_recv, chip_send, chip_recv):
+               lens_s, x_v, gain_v, wq_v, wk_v, wv_v, bq_v, bk_v, bv_v, cos_v, sin_v, part, pair_in, chip_in, direct_in, stat_out, stat_in,
+               w_sems, stat_send, stat_recv, pair_send, pair_recv, chip_send, chip_recv, direct_send, direct_recv):
     my = lax.axis_index("my")
     mx = lax.axis_index("mx")
     core, chip, partner, others = neighbours(mx)
     loads = [pltpu.make_async_copy(src, dst, w_sems.at[n]) for n, (src, dst) in enumerate((
         (wq_hbm, wq_v), (wk_hbm, wk_v), (wv_hbm, wv_v), (x_hbm, x_v), (gain_hbm, gain_v), (lens_hbm, lens_s), (bq_hbm, bq_v), (bk_hbm, bk_v), (bv_hbm, bv_v)))]
-    for n in (3, 4, 5, 0, 1, 2, 6, 7, 8):
-        loads[n].start()
-    enter(my, mx, False, loads[3].wait)
+    loads[3].start()
+
+    def meanwhile():
+        for n in (4, 5, 0, 1, 2, 6, 7, 8):
+            loads[n].start()
+        loads[3].wait()
+
+    enter(my, mx, False, meanwhile)
     x = x_v[...].astype(F32)
     square_sum = jnp.sum(x * x, axis=1, keepdims=True)
 
@@ -104,12 +113,17 @@
     biases = (bq_v, bk_v, bv_v)
     copies = []
     pair_copies = []
+    direct = []
     for n, (which, first, width, out_first) in enumerate(pieces):
         cols = pl.ds(out_first, width)
         product = jnp.dot(normed, weights[which][:, first:first + width], preferred_element_type=F32)
         part[:, :, :, cols] = product.reshape(4, 2, 8, width).astype(BF16)
-        pair_copies.append(send(part.at[:, 1 - core, :, cols], pair_in.at[:, :, cols], pair_send.at[n], pair_recv.at[n], my, partner))
-    for n, (which, first, width, out_first) in enumerate(pieces):
+        if n == 0:
+            for k, peer in enumerate(far_first(mx)):
+                direct.append(send(part.at[peer // 2, lax.rem(peer, 2), :, cols], direct_in.at[k], direct_send.at[k], direct_recv.at[k], my, peer))
+        else:
+            pair_copies.append(send(part.at[:, 1 - core, :, cols], pair_in.at[:, :, cols], pair_send.at[n - 1], pair_recv.at[n - 1], my, partner))
+    for n, (which, first, width, out_first) in enumerate(pieces[1:]):
         cols = pl.ds(out_first, width)
         pair_copies[n].wait_recv()
         pair_in[:, :, cols] = (part[:, core, :, cols].astype(F32) + pair_in[:, :, cols].astype(F32)).astype(BF16)
@@ -117,17 +131,23 @@
             copies.append(send(pair_in.at[other, :, cols], chip_in.at[k, :, cols], chip_send.at[n, k], chip_recv.at[n, k], my, other * 2 + core))
     for n, (which, first, width, out_first) in enumerate(pieces):
         cols = pl.ds(out_first, width)
-        total = pair_in[chip, :, cols].astype(F32)
-        for k in range(3):
-            copies[n * 3 + k].wait_recv()
-            total = total + chip_in[k, :, cols].astype(F32)
+        if n == 0:
+            total = part[chip, core, :, cols].astype(F32)
+            for k in range(7):
+                direct[k].wait_recv()
+                total = total + direct_in[k].astype(F32)
+        else:
+            total = pair_in[chip, :, cols].astype(F32)
+            for k in range(3):
+                copies[(n - 1) * 3 + k].wait_recv()
+                total = total + chip_in[k, :, cols].astype(F32)
         total = total + biases[which][first:first + width].astype(F32)[None, :]
         for h in range(0, width, HEAD):
             vals = total[:, h:h + HEAD]
             if which < 2:
                 vals = vals * cos_v[...] + pltpu.roll(vals, HEAD // 2, 1) * sin_v[...]
             out_ref[:, out_first + h:out_first + h + HEAD] = vals
-    for copy in pair_copies + copies:
+    for copy in direct + pair_copies + copies:
         copy.wait_send()
 
 
@@ -217,15 +237,14 @@
     y_pos = chip // 2
     x_peer = others[0] * 2 + core
     y_peer = others[1] * 2 + core
+    x_across = others[0] * 2 + (1 - core)
+    y_across = others[1] * 2 + (1 - core)
+    straight = chunks - 1
     half = 2 * act.shape[6]
     loads = chunks // per_load
     load_cols = per_load * 2 * half
     ring = wg_v.shape[0]
 
-    firsts = [pltpu.make_async_copy(src, dst, in_sems.at[n]) for n, (src, dst) in enumerate(((wo_hbm, wo_v), (x_hbm, x_v), (gain_hbm, gain_v)))]
-    for first in firsts:
-        first.start()
-
     def load_gate(n):
         cols = pl.ds(pl.multiple_of(n * load_cols, 128), load_cols)
         slot = lax.rem(n, ring)
@@ -234,37 +253,47 @@
     def load_down(n):
         return pltpu.make_async_copy(wd_hbm.at[n], wd_v.at[n], wd_sems.at[n])
 
-    @pl.loop(0, ring)
-    def _(n):
-        for load in load_gate(n):
-            load.start()
-
-    @pl.loop(0, loads)
-    def _(n):
-        load_down(n).start()
-
-    enter(my, mx, True)
+    firsts = [pltpu.make_async_copy(src, dst, in_sems.at[n]) for n, (src, dst) in enumerate(((wo_hbm, wo_v), (x_hbm, x_v), (gain_hbm, gain_v)))]
+
+    def meanwhile():
+        for first in firsts:
+            first.start()
+
+        @pl.loop(0, ring)
+        def _(n):
+            for load in load_gate(n):
+                load.start()
+
+        @pl.loop(0, loads)
+        def _(n):
+            load_down(n).start()
+
+        attn_all[mx] = attn_ref[...]
+        acc[...] = jnp.zeros_like(acc)
+
+    enter(my, mx, True, meanwhile)
 
     copies = []
-    for step in range(1, 8):
-        peer = lax.rem(mx + step, 8)
+    for step, peer in enumerate(far_first(mx)):
         copies.append(send(attn_ref, attn_all.at[mx], ag_send.at[step], ag_recv.at[step], my, peer))
-    attn_all[mx] = attn_ref[...]
     for first in firsts:
         first.wait()
     for copy in copies:
         copy.wait()
     rows = x_v.shape[0]
     attn = attn_all[...].reshape(rows, attn_ref.shape[1])
-    z_out[0] = jnp.dot(attn, wo_v[...], preferred_element_type=F32).astype(BF16)
-    z_copy = send(z_out.at[0], z_in.at[0], z_send.at[0], z_recv.at[0], 1 - my, mx)
-    z_copy.wait()
+    z_parts = (pl.ds(0, 384), pl.ds(384, x_v.shape[1] - 384))
+    z_copies = []
+    for n, part in enumerate(z_parts):
+        z_out[0, :, part] = jnp.dot(attn, wo_v[:, part], preferred_element_type=F32).astype(BF16)
+        z_copies.append(send(z_out.at[0, :, part], z_in.at[0, :, part], z_send.at[n], z_recv.at[n], 1 - my, mx))
+    for z_copy in z_copies:
+        z_copy.wait()
     mid = (x_v[...].astype(F32) + (z_out[0].astype(F32) + z_in[0].astype(F32))).astype(BF16)
     m_v[...] = mid
     mid = mid.astype(F32)
     stat = share_stat(jnp.sum(mid * mid, axis=1, keepdims=True), my, mx, stat_out, stat_in, stat_send, stat_recv)
     h_v[...] = (mid * lax.rsqrt(stat / hidden + NORM_EPS) * gain_v[...].astype(F32)[None, :]).astype(BF16)
-    acc[...] = jnp.zeros_like(acc)
 
     def multiply(k):
         n = k // per_load
@@ -326,10 +355,18 @@
         for block in (act.at[k, core, 0, 1 - y_pos, x_pos], act.at[k, core, 1, y_pos, 1 - x_pos]):
             send(block, block, fwd_send.at[k], fwd_recv.at[k], my, partner)
 
+        @pl.when(k >= straight)
+        def _():
+            for block, peer in ((act.at[k, core, 0, :, x_pos], x_across), (act.at[k, core, 1, y_pos], y_across)):
+                send(block, block, fwd_send.at[k], fwd_recv.at[k], my, peer)
+
     def forward(k):
         drain(act.at[k, core, 0], far_recv.at[k])
-        for block in (act.at[k, core, 0, :, 1 - x_pos], act.at[k, core, 1, 1 - y_pos]):
-            send(block, block, fwd_send.at[k], fwd_recv.at[k], my, partner)
+
+        @pl.when(k < straight)
+        def _():
+            for block in (act.at[k, core, 0, :, 1 - x_pos], act.at[k, core, 1, 1 - y_pos]):
+                send(block, block, fwd_send.at[k], fwd_recv.at[k], my, partner)
 
     def contract(k):
         n = k // per_load
@@ -346,9 +383,9 @@
             total = total + jnp.dot(lhs, wd_v[n, step, part], preferred_element_type=F32)
         acc[...] = total
 
-    stages = tuple(zip((contract, forward, gather, activate, combine, scatter, multiply), lags))
-
-    @pl.loop(0, chunks + lags[0])
+    stages = tuple(zip((forward, gather, activate, combine, scatter, contract, multiply), lags))
+
+    @pl.loop(0, chunks + max(lags))
     def _(t):
         for stage, lag in stages:
             @pl.when(jnp.logical_and(t >= lag, t < chunks + lag))
@@ -356,7 +393,7 @@
                 stage(t - lag)
 
     z_out[1] = acc[...].astype(BF16)
-    z_copy = send(z_out.at[1], z_in.at[1], z_send.at[1], z_recv.at[1], 1 - my, mx)
+    z_copy = send(z_out.at[1], z_in.at[1], z_send.at[2], z_recv.at[2], 1 - my, mx)
     z_copy.wait()
     out_ref[...] = (m_v[...].astype(F32) + (z_out[1].astype(F32) + z_in[1].astype(F32))).astype(BF16)
 
@@ -388,7 +425,9 @@
         kv_heads = kv_cols // HEAD
         local_rows = rows // mx_size
         qkv_cols = q_cols + 2 * kv_cols
-        pieces = ((0, 0, q_cols // 2, 0), (0, q_cols // 2, q_cols // 2, q_cols // 2), (1, 0, kv_cols, q_cols), (2, 0, kv_cols, q_cols + kv_cols))
+        first = 8 * HEAD
+        rest = (q_cols - first) // 2
+        pieces = ((0, 0, first, 0), (0, first, rest, first), (0, first + rest, rest, first + rest), (1, 0, kv_cols, q_cols), (2, 0, kv_cols, q_cols + kv_cols))
         inv_freq = ROPE_THETA ** (-2.0 * jnp.arange(HEAD // 2, dtype=F32) / HEAD)
 
         projected = pl.pallas_call(
@@ -401,9 +440,9 @@
                 pltpu.SMEM((local_rows,), jnp.int32), VMEM((rows, cols), BF16), VMEM((cols,), BF16),
                 VMEM(w_q.shape, BF16), VMEM(w_k.shape, BF16), VMEM(w_v.shape, BF16), VMEM(b_q.shape, BF16), VMEM(b_k.shape, BF16), VMEM(b_v.shape, BF16),
                 VMEM((local_rows, HEAD), F32), VMEM((local_rows, HEAD), F32),
-                VMEM((4, 2, local_rows, qkv_cols), BF16), VMEM((4, local_rows, qkv_cols), BF16), VMEM((3, local_rows, qkv_cols), BF16),
+                VMEM((4, 2, local_rows, qkv_cols), BF16), VMEM((4, local_rows, qkv_cols), BF16), VMEM((3, local_rows, qkv_cols), BF16), VMEM((7, local_rows, first), BF16),
                 VMEM((8, rows), F32), VMEM((8, 8, rows), F32),
-                DMA((9,)), DMA((8,)), DMA((8,)), DMA((4,)), DMA((4,)), DMA((4, 3)), DMA((4, 3)),
+                DMA((9,)), DMA((8,)), DMA((8,)), DMA((4,)), DMA((4,)), DMA((4, 3)), DMA((4, 3)), DMA((7,)), DMA((7,)),
             ],
             compiler_params=pltpu.CompilerParams(collective_id=0, has_side_effects=True, vmem_limit_bytes=16 * 2 ** 20),
             cost_estimate=pl.CostEstimate(flops=40_000_000_000, bytes_accessed=4_600_000, transcendentals=0),
@@ -434,7 +473,7 @@
         per_load = 1
         ring = 6
         loads = chunks // per_load
-        lags = (20, 17, 13, 9, 5, 2, 0)
+        lags = (17, 13, 9, 5, 2, 20, 0)
         x_out = pl.pallas_call(
             functools.partial(mlp_kernel, hidden, chunks, per_load, lags),
             name="mlp",
@@ -449,7 +488,7 @@
                 VMEM((rows, cols), BF16), VMEM((rows, cols), BF16), VMEM((rows, cols), F32),
             ] + [VMEM((chunks, 2, 2, 2, 2, 16, half // 2), BF16)] * 3 + [
                 VMEM((chunks, 2, 2, 2, 16, half // 2), BF16), VMEM((chunks, 2, 2, 16, half // 2), BF16), VMEM((chunks, 2, 2, 2, 2, 16, half // 2), BF16),
-                DMA((3,)), DMA((ring,)), DMA((ring,)), DMA((loads,)), DMA((8,)), DMA((8,)), DMA((2,)), DMA((2,)), DMA((8,)), DMA((8,)),
+                DMA((3,)), DMA((ring,)), DMA((ring,)), DMA((loads,)), DMA((8,)), DMA((8,)), DMA((3,)), DMA((3,)), DMA((8,)), DMA((8,)),
             ] + [DMA((chunks,))] * 12,
             compiler_params=pltpu.CompilerParams(collective_id=1, has_side_effects=True, vmem_limit_bytes=int(52.5 * 2 ** 20)),
             cost_estimate=pl.CostEstimate(flops=60_000_000_000, bytes_accessed=57_000_000, transcendentals=0),

time: 71.5 us -> 70.6 us (0.987)
  Pallas kernels: 70.1 us -> 69.1 us
where the time goes in v4:
time: 70.6 us; the launch traced here: 70.5 us
  Pallas kernels  69.1 us (98%)
    pallas_call x1, Pallas kernels, local_layer(): pl.pallas_call(functools.partial(mlp_kernel, hidden, chunks, per_load, la...  47.8 us
    pallas_call x1, Pallas kernels, local_layer(): pl.pallas_call(functools.partial(qkv_kernel, hidden, pieces), name='qkv',...  14.3 us
    pallas_call x1, Pallas kernels, local_layer(): pl.pallas_call(functools.partial(attend_kernel, heads), name='attend', ou...  7.02 us

profile of v4, /device:TPU:0, one launch (start us, length us, event | category | flops | bytes accessed | tf_op | source)
XLA Modules:
  0.0 70.5 jit_solution(1871164499759385905)
XLA Ops:
  0.6 0.0 copy-start
  0.7 0.0 copy-start.1
  0.7 14.3 %qkv.1.proj_ref = f32[8,3584]{1,0:T(8,128)S(1)} custom-call(f32[64]{0:T(128)S(1)} %multiply_power_fusion.freq_ref, s32[8]{0:T(128)} %lens_hbm.3, bf16[64,640]{1,0:T(8,128)(2,1)} %x_hbm.3, bf16[640]{0:T(1024)(128)(2,1)} %gain_hbm.2, bf16[640,2560]{1,0:T(8,128)(2,1)} %wq_hbm.1, bf16[640,512]{1,0:T(8,128)(2,1)} %wk_hbm.1, bf16[640,512]{1,0:T(8,128)(2,1)} %wv_hbm.1, ...), custom_call_target="tpu_custom_call" | custom-call | flops 40000000000 | bytes 4600000 | tf_op jit(solution)/shard_map/qkv/pallas_call | solution.py:433
  14.9 0.0 copy-done
  14.9 0.0 copy-done.1
  15.0 7.0 %attend.1 = (bf16[8,4096,128]{2,1,0:T(8,128)(2,1)}, bf16[8,4096,128]{2,1,0:T(8,128)(2,1)}, bf16[8,2560]{1,0:T(8,128)(2,1)S(1)}) custom-call(f32[8,3584]{1,0:T(8,128)S(1)} %qkv.1.proj_ref, bf16[8,4096,128]{2,1,0:T(8,128)(2,1)S(1)} %bitcast.5, bf16[8,4096,128]{2,1,0:T(8,128)(2,1)S(1)} %bitcast.6, s32[8]{0:T(128)} %lens_hbm.3), custom_call_target="tpu_custom_call" | custom-call | flops 20000000000 | bytes 17000000 | tf_op jit(solution)/shard_map/attend/pallas_call | solution.py:454
  22.0 47.8 %mlp.1 = bf16[64,640]{1,0:T(8,128)(2,1)S(1)} custom-call(bf16[8,2560]{1,0:T(8,128)(2,1)S(1)} %get-tuple-element.6.attn_ref, bf16[64,640]{1,0:T(8,128)(2,1)} %x_hbm.3, bf16[640]{0:T(1024)(128)(2,1)} %gain_hbm.3, bf16[2560,640]{1,0:T(8,128)(2,1)} %wo_hbm.1, bf16[640,13824]{1,0:T(8,128)(2,1)} %wg_hbm.1, bf16[640,13824]{1,0:T(8,128)(2,1)} %wu_hbm.1, ...), custom_call_target="tpu_custom_call" | custom-call | flops 60000002048 | bytes 57000000 | tf_op jit(solution)/shard_map/mlp/pallas_call | solution.py:477
  69.8 0.6 copy.20
  (1 shorter events, 0.0 us)
Async XLA Ops:
  0.6 14.3 %copy-start = (bf16[8,1024,4,128]{3,2,1,0:T(4,128)(2,1)S(1)}, bf16[8,1024,4,128]{3,2,1,0:T(4,128)(2,1)}, u32[]{:S(2)}) copy-start(bf16[8,1024,4,128]{3,2,1,0:T(4,128)(2,1)} %param.30) | copy-start | bytes 25165828
  0.7 14.3 %copy-start.1 = (bf16[8,1024,4,128]{3,2,1,0:T(4,128)(2,1)S(1)}, bf16[8,1024,4,128]{3,2,1,0:T(4,128)(2,1)}, u32[]{:S(2)}) copy-start(bf16[8,1024,4,128]{3,2,1,0:T(4,128)(2,1)} %param.31) | copy-start | bytes 25165828

commit v5 on v4

--- a/solution.py
+++ b/solution.py
@@ -473,7 +473,7 @@
         per_load = 1
         ring = 6
         loads = chunks // per_load
-        lags = (17, 13, 9, 5, 2, 20, 0)
+        lags = (21, 16, 11, 7, 2, 24, 0)
         x_out = pl.pallas_call(
             functools.partial(mlp_kernel, hidden, chunks, per_load, lags),
             name="mlp",

time: 70.6 us -> 70.3 us (level)
  no operation moved by 1% of the time
where the time goes in v5:
time: 70.3 us; the launch traced here: 70.2 us
  Pallas kernels  68.8 us (98%)
    pallas_call x1, Pallas kernels, local_layer(): pl.pallas_call(functools.partial(mlp_kernel, hidden, chunks, per_load, la...  47.6 us
    pallas_call x1, Pallas kernels, local_layer(): pl.pallas_call(functools.partial(qkv_kernel, hidden, pieces), name='qkv',...  14.3 us
    pallas_call x1, Pallas kernels, local_layer(): pl.pallas_call(functools.partial(attend_kernel, heads), name='attend', ou...  7.02 us

profile of v5, /device:TPU:0, one launch (start us, length us, event | category | flops | bytes accessed | tf_op | source)
XLA Modules:
  0.0 70.2 jit_solution(2710388300612407524)
XLA Ops:
  0.6 0.0 copy-start
  0.7 0.0 copy-start.1
  0.7 14.3 %qkv.1.proj_ref = f32[8,3584]{1,0:T(8,128)S(1)} custom-call(f32[64]{0:T(128)S(1)} %multiply_power_fusion.freq_ref, s32[8]{0:T(128)} %lens_hbm.3, bf16[64,640]{1,0:T(8,128)(2,1)} %x_hbm.3, bf16[640]{0:T(1024)(128)(2,1)} %gain_hbm.2, bf16[640,2560]{1,0:T(8,128)(2,1)} %wq_hbm.1, bf16[640,512]{1,0:T(8,128)(2,1)} %wk_hbm.1, bf16[640,512]{1,0:T(8,128)(2,1)} %wv_hbm.1, ...), custom_call_target="tpu_custom_call" | custom-call | flops 40000000000 | bytes 4600000 | tf_op jit(solution)/shard_map/qkv/pallas_call | solution.py:433
  14.9 0.0 copy-done
  14.9 0.0 copy-done.1
  15.0 7.0 %attend.1 = (bf16[8,4096,128]{2,1,0:T(8,128)(2,1)}, bf16[8,4096,128]{2,1,0:T(8,128)(2,1)}, bf16[8,2560]{1,0:T(8,128)(2,1)S(1)}) custom-call(f32[8,3584]{1,0:T(8,128)S(1)} %qkv.1.proj_ref, bf16[8,4096,128]{2,1,0:T(8,128)(2,1)S(1)} %bitcast.5, bf16[8,4096,128]{2,1,0:T(8,128)(2,1)S(1)} %bitcast.6, s32[8]{0:T(128)} %lens_hbm.3), custom_call_target="tpu_custom_call" | custom-call | flops 20000000000 | bytes 17000000 | tf_op jit(solution)/shard_map/attend/pallas_call | solution.py:454
  22.0 47.6 %mlp.1 = bf16[64,640]{1,0:T(8,128)(2,1)S(1)} custom-call(bf16[8,2560]{1,0:T(8,128)(2,1)S(1)} %get-tuple-element.6.attn_ref, bf16[64,640]{1,0:T(8,128)(2,1)} %x_hbm.3, bf16[640]{0:T(1024)(128)(2,1)} %gain_hbm.3, bf16[2560,640]{1,0:T(8,128)(2,1)} %wo_hbm.1, bf16[640,13824]{1,0:T(8,128)(2,1)} %wg_hbm.1, bf16[640,13824]{1,0:T(8,128)(2,1)} %wu_hbm.1, ...), custom_call_target="tpu_custom_call" | custom-call | flops 60000002048 | bytes 57000000 | tf_op jit(solution)/shard_map/mlp/pallas_call | solution.py:477
  69.6 0.6 copy.20
  (1 shorter events, 0.0 us)
Async XLA Ops:
  0.6 14.3 %copy-start = (bf16[8,1024,4,128]{3,2,1,0:T(4,128)(2,1)S(1)}, bf16[8,1024,4,128]{3,2,1,0:T(4,128)(2,1)}, u32[]{:S(2)}) copy-start(bf16[8,1024,4,128]{3,2,1,0:T(4,128)(2,1)} %param.30) | copy-start | bytes 25165828
  0.7 14.3 %copy-start.1 = (bf16[8,1024,4,128]{3,2,1,0:T(4,128)(2,1)S(1)}, bf16[8,1024,4,128]{3,2,1,0:T(4,128)(2,1)}, u32[]{:S(2)}) copy-start(bf16[8,1024,4,128]{3,2,1,0:T(4,128)(2,1)} %param.31) | copy-start | bytes 25165828

commit v6 on v5

--- a/solution.py
+++ b/solution.py
@@ -273,12 +273,22 @@
 
     enter(my, mx, True, meanwhile)
 
-    copies = []
-    for step, peer in enumerate(far_first(mx)):
-        copies.append(send(attn_ref, attn_all.at[mx], ag_send.at[step], ag_recv.at[step], my, peer))
+    others = (others[2], others[0], others[1])
+    shared = pl.ds(0, 12 * HEAD)
+    direct = pl.ds(12 * HEAD, attn_ref.shape[1] - 12 * HEAD)
+    spread = [send(attn_ref.at[:, shared], attn_all.at[mx, :, shared], ag_send.at[k], ag_recv.at[k], my, other * 2 + core) for k, other in enumerate(others)]
+    passed = [send(attn_ref, attn_all.at[mx], ag_send.at[3], ag_recv.at[3], my, partner)]
+    for k, other in enumerate(others):
+        for n, peer in enumerate((other * 2 + core, other * 2 + (1 - core))):
+            slot = 4 + 2 * k + n
+            passed.append(send(attn_ref.at[:, direct], attn_all.at[mx, :, direct], ag_send.at[slot], ag_recv.at[slot], my, peer))
+    for k, other in enumerate(others):
+        spread[k].wait()
+        block = attn_all.at[other * 2 + core, :, shared]
+        passed.append(send(block, block, ag_send.at[10 + k], ag_recv.at[10 + k], my, partner))
     for first in firsts:
         first.wait()
-    for copy in copies:
+    for copy in passed:
         copy.wait()
     rows = x_v.shape[0]
     attn = attn_all[...].reshape(rows, attn_ref.shape[1])
@@ -488,7 +498,7 @@
                 VMEM((rows, cols), BF16), VMEM((rows, cols), BF16), VMEM((rows, cols), F32),
             ] + [VMEM((chunks, 2, 2, 2, 2, 16, half // 2), BF16)] * 3 + [
                 VMEM((chunks, 2, 2, 2, 16, half // 2), BF16), VMEM((chunks, 2, 2, 16, half // 2), BF16), VMEM((chunks, 2, 2, 2, 2, 16, half // 2), BF16),
-                DMA((3,)), DMA((ring,)), DMA((ring,)), DMA((loads,)), DMA((8,)), DMA((8,)), DMA((3,)), DMA((3,)), DMA((8,)), DMA((8,)),
+                DMA((3,)), DMA((ring,)), DMA((ring,)), DMA((loads,)), DMA((13,)), DMA((13,)), DMA((3,)), DMA((3,)), DMA((8,)), DMA((8,)),
             ] + [DMA((chunks,))] * 12,
             compiler_params=pltpu.CompilerParams(collective_id=1, has_side_effects=True, vmem_limit_bytes=int(52.5 * 2 ** 20)),
             cost_estimate=pl.CostEstimate(flops=60_000_000_000, bytes_accessed=57_000_000, transcendentals=0),

time: 70.3 us -> 70.1 us (level)
  no operation moved by 1% of the time
where the time goes in v6:
time: 70.1 us; the launch traced here: 70 us
  Pallas kernels  68.7 us (98%)
    pallas_call x1, Pallas kernels, local_layer(): pl.pallas_call(functools.partial(mlp_kernel, hidden, chunks, per_load, la...  47.4 us
    pallas_call x1, Pallas kernels, local_layer(): pl.pallas_call(functools.partial(qkv_kernel, hidden, pieces), name='qkv',...  14.3 us
    pallas_call x1, Pallas kernels, local_layer(): pl.pallas_call(functools.partial(attend_kernel, heads), name='attend', ou...  7.02 us

profile of v6, /device:TPU:0, one launch (start us, length us, event | category | flops | bytes accessed | tf_op | source)
XLA Modules:
  0.0 70.0 jit_solution(16173137435747368478)
XLA Ops:
  0.6 0.0 copy-start
  0.7 0.0 copy-start.1
  0.7 14.3 %qkv.1.proj_ref = f32[8,3584]{1,0:T(8,128)S(1)} custom-call(f32[64]{0:T(128)S(1)} %multiply_power_fusion.freq_ref, s32[8]{0:T(128)} %lens_hbm.3, bf16[64,640]{1,0:T(8,128)(2,1)} %x_hbm.3, bf16[640]{0:T(1024)(128)(2,1)} %gain_hbm.2, bf16[640,2560]{1,0:T(8,128)(2,1)} %wq_hbm.1, bf16[640,512]{1,0:T(8,128)(2,1)} %wk_hbm.1, bf16[640,512]{1,0:T(8,128)(2,1)} %wv_hbm.1, ...), custom_call_target="tpu_custom_call" | custom-call | flops 40000000000 | bytes 4600000 | tf_op jit(solution)/shard_map/qkv/pallas_call | solution.py:443
  14.9 0.0 copy-done
  14.9 0.0 copy-done.1
  15.0 7.0 %attend.1 = (bf16[8,4096,128]{2,1,0:T(8,128)(2,1)}, bf16[8,4096,128]{2,1,0:T(8,128)(2,1)}, bf16[8,2560]{1,0:T(8,128)(2,1)S(1)}) custom-call(f32[8,3584]{1,0:T(8,128)S(1)} %qkv.1.proj_ref, bf16[8,4096,128]{2,1,0:T(8,128)(2,1)S(1)} %bitcast.5, bf16[8,4096,128]{2,1,0:T(8,128)(2,1)S(1)} %bitcast.6, s32[8]{0:T(128)} %lens_hbm.3), custom_call_target="tpu_custom_call" | custom-call | flops 20000000000 | bytes 17000000 | tf_op jit(solution)/shard_map/attend/pallas_call | solution.py:464
  22.0 47.4 %mlp.1 = bf16[64,640]{1,0:T(8,128)(2,1)S(1)} custom-call(bf16[8,2560]{1,0:T(8,128)(2,1)S(1)} %get-tuple-element.6.attn_ref, bf16[64,640]{1,0:T(8,128)(2,1)} %x_hbm.3, bf16[640]{0:T(1024)(128)(2,1)} %gain_hbm.3, bf16[2560,640]{1,0:T(8,128)(2,1)} %wo_hbm.1, bf16[640,13824]{1,0:T(8,128)(2,1)} %wg_hbm.1, bf16[640,13824]{1,0:T(8,128)(2,1)} %wu_hbm.1, ...), custom_call_target="tpu_custom_call" | custom-call | flops 60000002048 | bytes 57000000 | tf_op jit(solution)/shard_map/mlp/pallas_call | solution.py:487
  69.4 0.6 copy.20
  (1 shorter events, 0.0 us)
Async XLA Ops:
  0.6 14.3 %copy-start = (bf16[8,1024,4,128]{3,2,1,0:T(4,128)(2,1)S(1)}, bf16[8,1024,4,128]{3,2,1,0:T(4,128)(2,1)}, u32[]{:S(2)}) copy-start(bf16[8,1024,4,128]{3,2,1,0:T(4,128)(2,1)} %param.30) | copy-start | bytes 25165828
  0.7 14.3 %copy-start.1 = (bf16[8,1024,4,128]{3,2,1,0:T(4,128)(2,1)S(1)}, bf16[8,1024,4,128]{3,2,1,0:T(4,128)(2,1)}, u32[]{:S(2)}) copy-start(bf16[8,1024,4,128]{3,2,1,0:T(4,128)(2,1)} %param.31) | copy-start | bytes 25165828

commit v7 on v6

--- a/solution.py
+++ b/solution.py
@@ -483,7 +483,7 @@
         per_load = 1
         ring = 6
         loads = chunks // per_load
-        lags = (21, 16, 11, 7, 2, 24, 0)
+        lags = (20, 15, 10, 6, 2, 23, 0)
         x_out = pl.pallas_call(
             functools.partial(mlp_kernel, hidden, chunks, per_load, lags),
             name="mlp",

time: 70.1 us -> 69.9 us (level)
  no operation moved by 1% of the time
where the time goes in v7:
time: 69.9 us; the launch traced here: 69.8 us
  Pallas kernels  68.4 us (98%)
    pallas_call x1, Pallas kernels, local_layer(): pl.pallas_call(functools.partial(mlp_kernel, hidden, chunks, per_load, la...  47.2 us
    pallas_call x1, Pallas kernels, local_layer(): pl.pallas_call(functools.partial(qkv_kernel, hidden, pieces), name='qkv',...  14.3 us
    pallas_call x1, Pallas kernels, local_layer(): pl.pallas_call(functools.partial(attend_kernel, heads), name='attend', ou...  7.02 us

profile of v7, /device:TPU:0, one launch (start us, length us, event | category | flops | bytes accessed | tf_op | source)
XLA Modules:
  0.0 69.8 jit_solution(3649069340202730572)
XLA Ops:
  0.6 0.0 copy-start
  0.7 0.0 copy-start.1
  0.7 14.3 %qkv.1.proj_ref = f32[8,3584]{1,0:T(8,128)S(1)} custom-call(f32[64]{0:T(128)S(1)} %multiply_power_fusion.freq_ref, s32[8]{0:T(128)} %lens_hbm.3, bf16[64,640]{1,0:T(8,128)(2,1)} %x_hbm.3, bf16[640]{0:T(1024)(128)(2,1)} %gain_hbm.2, bf16[640,2560]{1,0:T(8,128)(2,1)} %wq_hbm.1, bf16[640,512]{1,0:T(8,128)(2,1)} %wk_hbm.1, bf16[640,512]{1,0:T(8,128)(2,1)} %wv_hbm.1, ...), custom_call_target="tpu_custom_call" | custom-call | flops 40000000000 | bytes 4600000 | tf_op jit(solution)/shard_map/qkv/pallas_call | solution.py:443
  14.9 0.0 copy-done
  14.9 0.0 copy-done.1
  15.0 7.0 %attend.1 = (bf16[8,4096,128]{2,1,0:T(8,128)(2,1)}, bf16[8,4096,128]{2,1,0:T(8,128)(2,1)}, bf16[8,2560]{1,0:T(8,128)(2,1)S(1)}) custom-call(f32[8,3584]{1,0:T(8,128)S(1)} %qkv.1.proj_ref, bf16[8,4096,128]{2,1,0:T(8,128)(2,1)S(1)} %bitcast.5, bf16[8,4096,128]{2,1,0:T(8,128)(2,1)S(1)} %bitcast.6, s32[8]{0:T(128)} %lens_hbm.3), custom_call_target="tpu_custom_call" | custom-call | flops 20000000000 | bytes 17000000 | tf_op jit(solution)/shard_map/attend/pallas_call | solution.py:464
  22.0 47.2 %mlp.1 = bf16[64,640]{1,0:T(8,128)(2,1)S(1)} custom-call(bf16[8,2560]{1,0:T(8,128)(2,1)S(1)} %get-tuple-element.6.attn_ref, bf16[64,640]{1,0:T(8,128)(2,1)} %x_hbm.3, bf16[640]{0:T(1024)(128)(2,1)} %gain_hbm.3, bf16[2560,640]{1,0:T(8,128)(2,1)} %wo_hbm.1, bf16[640,13824]{1,0:T(8,128)(2,1)} %wg_hbm.1, bf16[640,13824]{1,0:T(8,128)(2,1)} %wu_hbm.1, ...), custom_call_target="tpu_custom_call" | custom-call | flops 60000002048 | bytes 57000000 | tf_op jit(solution)/shard_map/mlp/pallas_call | solution.py:487
  69.1 0.6 copy.20
  (1 shorter events, 0.0 us)
Async XLA Ops:
  0.6 14.3 %copy-start = (bf16[8,1024,4,128]{3,2,1,0:T(4,128)(2,1)S(1)}, bf16[8,1024,4,128]{3,2,1,0:T(4,128)(2,1)}, u32[]{:S(2)}) copy-start(bf16[8,1024,4,128]{3,2,1,0:T(4,128)(2,1)} %param.30) | copy-start | bytes 25165828
  0.7 14.3 %copy-start.1 = (bf16[8,1024,4,128]{3,2,1,0:T(4,128)(2,1)S(1)}, bf16[8,1024,4,128]{3,2,1,0:T(4,128)(2,1)}, u32[]{:S(2)}) copy-start(bf16[8,1024,4,128]{3,2,1,0:T(4,128)(2,1)} %param.31) | copy-start | bytes 25165828
